TPU v7x, 128 devices: a whole 4x4x4 slice. The times are simulated.
128 devices in a mesh: member: 2 (over x_lo), fsdp: 64 (over z, y, x_hi, core).
Axes of the slice: x: 4 (x_hi: 2, x_lo: 2; x = x_hi * 2 + x_lo), y: 4, z: 4, core: 2. Of those that a mesh axis runs over, the one named last changes fastest.
Arguments:
- latents: bfloat16 [2, 131072, 512], P('member', 'fsdp'), may hold values from -16 to 16
- noise: float32 [2, 32], P('member'), may hold values from -4 to 4
- cond_gain: float32 [32, 512], replicated, may hold values from -0.5 to 0.5
- cond_shift: float32 [32, 512], replicated, may hold values from -0.5 to 0.5
- w_in: bfloat16 [512, 2048], P('fsdp'), may hold values from -0.25 to 0.25
- b_in: float32 [2048], replicated, may hold values from -3 to 3
- w_out: bfloat16 [2048, 512], P('fsdp'), may hold values from -0.125 to 0.125
- target: bfloat16 [131072, 512], P('fsdp'), may hold values from -6 to 6
Outputs:
- prediction: bfloat16 [2, 131072, 512], P('member', 'fsdp')
- grad_in: float32 [512, 2048], P('fsdp')
- grad_out: float32 [2048, 512], P('fsdp')
- crps_mean: float32 [], replicated
All inputs are finite; a program needn't handle non-finite values.
Results may differ from a plain program's by a relative error of at most 0.0043.
Values may be sent and summed in bfloat16 or wider, within the bound.
A program may use at most 128 MiB of HBM per device.

v0:
```python
import functools

import jax
import jax.numpy as jnp
from jax import lax
from jax.sharding import Mesh
from jax.sharding import PartitionSpec as P

FSDP = ("fsdp_0", "fsdp_1", "fsdp_2", "fsdp_3")
MEMBER_FSDP = ("member", "fsdp_0", "fsdp_1", "fsdp_2", "fsdp_3")


COEF = 0.7978845608
CUBIC = 0.044715


def swapped(block, axis, apart):
    count = lax.axis_size(axis)
    route = []
    for low in range(count):
        high = low | 1 << apart
        if high != low and high < count:
            route += [(low, high), (high, low)]
    return lax.ppermute(block, axis, route)


def over_axes(x, axes):
    return functools.reduce(lax.psum, axes, x)


def total_of_pieces(x, axis):
    return lax.all_gather(x, axis).astype(jnp.float32).sum(0)


def in_blocks(x, dim, count):
    before, after = (x.shape[:dim], x.shape[dim + 1 :])
    return jnp.moveaxis(x.reshape(*before, count, -1, *after), dim, 0)


def sum_at_owner(x, axis, dim):
    count = lax.axis_size(axis)
    tiles = lax.all_to_all(in_blocks(x, dim, count), axis, 0, 0, tiled=True)
    return jnp.sum(tiles.astype(jnp.float32), axis=0)


def gelu_value(v):
    return 0.5 * v * (1.0 + jnp.tanh(COEF * (v + CUBIC * v * v * v)))


def gelu_slope(v):
    u = jnp.tanh(COEF * (v + CUBIC * v * v * v))
    return 0.5 * (1.0 + u) + 0.5 * v * (1.0 - u * u) * COEF * (1.0 + 3.0 * CUBIC * v * v)


def smooth(d):
    return jnp.sqrt(d * d + 0.0625)


def on_device(latents, noise, cond_gain, cond_shift, w_in, b_in, w_out, target):
    block = latents[0]
    noise_row = noise[0]
    rows = block.shape[0]
    width = block.shape[1]
    groups = lax.axis_size(FSDP)
    nodes = rows * groups
    gain = (
        1.0
        + jnp.dot(
            noise_row[None, :],
            cond_gain,
            precision=lax.Precision.HIGHEST,
            preferred_element_type=jnp.float32,
        )[0]
    )
    shift = jnp.dot(
        noise_row[None, :],
        cond_shift,
        precision=lax.Precision.HIGHEST,
        preferred_element_type=jnp.float32,
    )[0]
    values = block.astype(jnp.float32)
    center = jnp.mean(values, axis=1, keepdims=True)
    spread = jnp.mean((values - center) ** 2, axis=1, keepdims=True)
    normed = ((values - center) / jnp.sqrt(spread + 0.25) * gain + shift).astype(jnp.bfloat16)
    columns = normed
    pre = (
        jnp.dot(
            columns,
            lax.all_gather(w_in, FSDP, axis=0, tiled=True),
            preferred_element_type=jnp.float32,
        )
        + b_in
    )
    act = gelu_value(pre).astype(jnp.bfloat16)
    columns = act
    output = values + jnp.dot(
        columns, lax.all_gather(w_out, FSDP, axis=0, tiled=True), preferred_element_type=jnp.float32
    )
    prediction = output.astype(jnp.bfloat16)
    partner = swapped(prediction, "member", 0)
    mine = prediction.astype(jnp.float32)
    near = mine - target.astype(jnp.float32)
    apart = mine - partner.astype(jnp.float32)
    local_sum = jnp.sum(0.5 * smooth(near) - 0.25 * smooth(apart))
    crps_mean = over_axes(local_sum, MEMBER_FSDP) / jnp.float32(2 * nodes * width)
    scale = 1.0 / jnp.sqrt(jnp.float32(2 * nodes))
    dpred = ((0.5 * near / smooth(near) - 0.5 * apart / smooth(apart)) * scale).astype(jnp.bfloat16)
    across = (((1,), (1,)), ((), ()))
    dact = lax.dot_general(
        dpred,
        lax.all_gather(w_out, FSDP, axis=0, tiled=True),
        across,
        preferred_element_type=jnp.float32,
    )
    dpre = (dact * gelu_slope(pre)).astype(jnp.bfloat16)
    contract = (((0,), (0,)), ((), ()))
    full_in = lax.dot_general(normed, dpre, contract, preferred_element_type=jnp.float32)
    full_out = lax.dot_general(act, dpred, contract, preferred_element_type=jnp.float32)
    paired_in, paired_out = (
        total_of_pieces(full_in.astype(jnp.bfloat16), "member").astype(jnp.float32),
        total_of_pieces(full_out.astype(jnp.bfloat16), "member").astype(jnp.float32),
    )
    grad_in, grad_out = (
        sum_at_owner(paired_in.astype(jnp.bfloat16), FSDP, 0),
        sum_at_owner(paired_out.astype(jnp.bfloat16), FSDP, 0),
    )
    return (prediction[None], grad_in, grad_out, crps_mean)


def solution(mesh):
    torus = Mesh(
        mesh.devices.reshape(mesh.shape["member"], 4, 4, 2, 2),
        ("member", "fsdp_0", "fsdp_1", "fsdp_2", "fsdp_3"),
    )
    in_specs = (
        P("member", FSDP, None),
        P("member", None),
        P(),
        P(),
        P(FSDP, None),
        P(),
        P(FSDP, None),
        P(FSDP, None),
    )
    out_specs = (P("member", FSDP, None), P(FSDP, None), P(FSDP, None), P())
    return jax.shard_map(
        on_device, mesh=torus, in_specs=in_specs, out_specs=out_specs, check_vma=False
    )
```

profile of v0, /device:TPU:0, one launch (start us, length us, event | category | flops | bytes accessed | tf_op | source)
XLA Modules:
  0.0 459.8 jit_solution(7178948828208920969)
XLA Ops:
  8.8 1.9 convert_reduce_fusion
  11.5 2.5 fusion.12
  14.2 67.6 %all-gather.7.cloned.1.call-done = bf16[512,2048]{1,0:T(8,128)(2,1)} async-done(((bf16[8,2048]{1,0:T(8,128)(2,1)}), bf16[512,2048]{1,0:T(8,128)(2,1)}) %all-gather.7.cloned.1.call-update) | async-done | bytes 2097168 | tf_op jit(solution)/shard_map/all_gather | solution.py:89
  81.8 13.7 %multiply_convert_fusion = (bf16[2048,2048]{1,0:T(8,128)(2,1)}, f32[2048,2048]{1,0:T(8,128)}) fusion(f32[2048]{0:T(1024)S(1)} %copy-done.6, bf16[512,2048]{1,0:T(8,128)(2,1)} %all-gather.7.cloned.1.call-done, bf16[1,2048,512]{2,1,0:T(8,128)(2,1)S(1)} %copy-done.1, f32[512]{0:T(512)S(1)} %bitcast.49, f32[512]{0:T(512)S(1)} %broadcast_add_fusion, ...), kind=kOutput, calls=%fused_computation.9 | convolution fusion | flops 4343201792 | bytes 29388800 | tf_op jit(solution)/shard_map/dot_general | solution.py:87
  95.5 54.5 %all-gather.9.cloned.1.call-done = bf16[2048,512]{1,0:T(8,128)(2,1)} async-done(((bf16[32,512]{1,0:T(8,128)(2,1)}), bf16[2048,512]{1,0:T(8,128)(2,1)}) %all-gather.9.cloned.1.call-update) | async-done | bytes 2097168 | tf_op jit(solution)/shard_map/all_gather | solution.py:97
  150.0 8.5 %fusion.16 = bf16[2048,512]{1,0:T(8,128)(2,1)S(1)} fusion(bf16[1,2048,512]{2,1,0:T(8,128)(2,1)S(1)} %copy-done.1, bf16[2048,2048]{1,0:T(8,128)(2,1)} %get-tuple-element.4, bf16[2048,512]{1,0:T(8,128)(2,1)} %all-gather.9.cloned.1.call-done), kind=kOutput, calls=%fused_computation.23 | convolution fusion | flops 4298113024 | bytes 14680064 | tf_op jit(solution)/shard_map/dot_general | solution.py:96
  158.5 1.3 copy-done.2
  160.4 47.2 %collective-permute-done = bf16[2048,512]{1,0:T(8,128)(2,1)S(1)} collective-permute-done((bf16[2048,512]{1,0:T(8,128)(2,1)S(1)}, bf16[2048,512]{1,0:T(8,128)(2,1)S(1)}, u32[]{:S(2)}, u32[]{:S(2)}) %collective-permute-start) | collective-permute-done | bytes 2097184 | tf_op jit(solution)/shard_map/ppermute | solution.py:24
  207.6 1.4 copy-done.3
  209.0 26.8 %fusion.17 = bf16[512,2048]{1,0:T(8,128)(2,1)} fusion(f32[2048,2048]{1,0:T(8,128)} %get-tuple-element.5, bf16[2048,512]{1,0:T(8,128)(2,1)} %all-gather.9.cloned.1.call-done, f32[2048]{0:T(1024)S(1)} %copy-done.6, bf16[1,2048,512]{2,1,0:T(8,128)(2,1)S(1)} %copy-done.1, f32[512]{0:T(512)S(1)} %bitcast.50, f32[512]{0:T(512)S(1)} %broadcast_add_fusion, ...), kind=kOutput, calls=%fused_computation.30 | convolution fusion | flops 8697937920 | bytes 29388800 | tf_op jit(solution)/shard_map/dot_general | solution.py:117
  236.1 13.9 %convolution_convert_fusion = bf16[2048,512]{1,0:T(8,128)(2,1)} fusion(bf16[2048,2048]{1,0:T(8,128)(2,1)} %get-tuple-element.4, bf16[2048,512]{1,0:T(8,128)(2,1)} %param.15, bf16[2048,512]{1,0:T(8,128)(2,1)} %copy-done.2, bf16[2048,512]{1,0:T(8,128)(2,1)} %copy-done.3), kind=kOutput, calls=%fused_computation.31 | convolution fusion | flops 4312793088 | bytes 16777216 | tf_op jit(solution)/shard_map/dot_general | solution.py:118
  250.0 42.1 %all-gather.11.cloned.1.call-done = bf16[1024,2048]{1,0:T(8,128)(2,1)} async-done(((bf16[512,2048]{1,0:T(8,128)(2,1)}), bf16[1024,2048]{1,0:T(8,128)(2,1)}) %all-gather.11.cloned.1.call-update) | async-done | bytes 4194320 | tf_op jit(solution)/shard_map/all_gather | solution.py:32
  292.1 5.1 %reduce_sum.71 = bf16[512,2048]{1,0:T(8,128)(2,1)} reduce(bf16[2,512,2048]{2,1,0:T(8,128)(2,1)} %bitcast.45, bf16[]{:T(256)} %constant.28.clone.1), dimensions={0}, to_apply=%region_2.0 | reduce | flops 1048576 | bytes 6291458 | tf_op jit(solution)/shard_map/reduce_sum | solution.py:32
  297.1 10.0 %all-to-all-start = ((bf16[64,8,2048]{2,1,0:T(8,128)(2,1)}), bf16[64,8,2048]{2,1,0:T(8,128)(2,1)S(1)}, u32[]{:S(2)}, u32[]{:S(2)}) async-start(bf16[64,8,2048]{2,1,0:T(8,128)(2,1)} %bitcast.8), calls=%async_computation | async-start | bytes 4194304 | tf_op jit(solution)/shard_map/all_to_all | solution.py:42
  307.1 68.7 %all-gather.13.cloned.1.call-done = bf16[4096,512]{1,0:T(8,128)(2,1)} async-done(((bf16[2048,512]{1,0:T(8,128)(2,1)}), bf16[4096,512]{1,0:T(8,128)(2,1)}) %all-gather.13.cloned.1.call-update) | async-done | bytes 4194320 | tf_op jit(solution)/shard_map/all_gather | solution.py:32
  375.8 5.0 %reduce_sum.73 = bf16[2048,512]{1,0:T(8,128)(2,1)} reduce(bf16[2,2048,512]{2,1,0:T(8,128)(2,1)} %bitcast.46, bf16[]{:T(256)} %constant.28.clone.1), dimensions={0}, to_apply=%region_4.0 | reduce | flops 1048576 | bytes 6291458 | tf_op jit(solution)/shard_map/reduce_sum | solution.py:32
  380.8 10.8 %all-to-all-start.1 = ((bf16[64,32,512]{2,1,0:T(8,128)(2,1)}), bf16[64,32,512]{2,1,0:T(8,128)(2,1)}, u32[]{:S(2)}, u32[]{:S(2)}) async-start(bf16[64,32,512]{2,1,0:T(8,128)(2,1)} %bitcast.10), calls=%async_computation.1 | async-start | bytes 4194304 | tf_op jit(solution)/shard_map/all_to_all | solution.py:42
  391.5 7.1 %subtract_reduce_fusion = f32[]{:T(128)} fusion(bf16[2048,512]{1,0:T(8,128)(2,1)} %param.15, bf16[2048,512]{1,0:T(8,128)(2,1)} %copy-done.2, bf16[2048,512]{1,0:T(8,128)(2,1)} %copy-done.3), kind=kLoop, calls=%fused_computation.24 | loop fusion | flops 13631487 | bytes 6291460 | tf_op jit(solution)/shard_map/reduce_sum | solution.py:104
  398.7 16.7 %psum.35 = f32[]{:T(128)} all-reduce(f32[]{:T(128)} %subtract_reduce_fusion), channel_id=1, replica_groups=mesh['member'=2,'fsdp_0'=4,'fsdp_1'=4,'fsdp_2'=2,'fsdp_3'=2] {'member'}, use_global_device_ids=true, to_apply=%region_7.0 | all-reduce | flops 1 | bytes 8 | tf_op jit(solution)/shard_map/psum | solution.py:28
  415.3 11.4 %psum.36 = f32[]{:T(128)} all-reduce(f32[]{:T(128)} %psum.35), channel_id=1, replica_groups=mesh['member'=2,'fsdp_0'=4,'fsdp_1'=4,'fsdp_2'=2,'fsdp_3'=2] {'fsdp_0'}, use_global_device_ids=true, to_apply=%region_8.0 | all-reduce | flops 1 | bytes 8 | tf_op jit(solution)/shard_map/psum | solution.py:28
  426.7 11.1 %psum.37 = f32[]{:T(128)} all-reduce(f32[]{:T(128)} %psum.36), channel_id=1, replica_groups=mesh['member'=2,'fsdp_0'=4,'fsdp_1'=4,'fsdp_2'=2,'fsdp_3'=2] {'fsdp_1'}, use_global_device_ids=true, to_apply=%region_9.0 | all-reduce | flops 1 | bytes 8 | tf_op jit(solution)/shard_map/psum | solution.py:28
  437.8 7.1 %psum.38 = f32[]{:T(128)} all-reduce(f32[]{:T(128)} %psum.37), channel_id=1, replica_groups=mesh['member'=2,'fsdp_0'=4,'fsdp_1'=4,'fsdp_2'=2,'fsdp_3'=2] {'fsdp_2'}, use_global_device_ids=true, to_apply=%region_10.0 | all-reduce | flops 1 | bytes 8 | tf_op jit(solution)/shard_map/psum | solution.py:28
  444.9 3.1 psum.39
  449.6 2.5 convert_reduce_fusion.1
  (29 shorter events, 4.3 us)
Async XLA Ops:
  7.2 3.5 copy-start
  7.2 74.6 %copy-start.1 = (bf16[1,2048,512]{2,1,0:T(8,128)(2,1)S(1)}, bf16[1,2048,512]{2,1,0:T(8,128)(2,1)}, u32[]{:S(2)}) copy-start(bf16[1,2048,512]{2,1,0:T(8,128)(2,1)} %param.8) | copy-start | bytes 6291460
  7.2 6.9 %copy-start.5 = (f32[1,32]{1,0:T(1,128)S(1)}, f32[1,32]{1,0:T(1,128)}, u32[]{:S(2)}) copy-start(f32[1,32]{1,0:T(1,128)} %param.9) | copy-start | bytes 388
  7.2 6.8 %copy-start.4 = (f32[32,512]{1,0:T(8,128)S(1)}, f32[32,512]{1,0:T(8,128)}, u32[]{:S(2)}) copy-start(f32[32,512]{1,0:T(8,128)} %param.11) | copy-start | bytes 196612
  7.2 74.6 %copy-start.6 = (f32[2048]{0:T(1024)S(1)}, f32[2048]{0:T(1024)}, u32[]{:S(2)}) copy-start(f32[2048]{0:T(1024)} %param.13) | copy-start | bytes 24580
  7.2 74.6 %all-gather.7.cloned.1.call-start = ((), (), s32[]{:S(2)}) async-start(), calls=%async_computation.2 | async-start | bytes 2129920 | tf_op jit(solution)/shard_map/all_gather | solution.py:89
  8.0 142.0 %all-gather.9.cloned.1.call-start = ((), (), s32[]{:S(2)}) async-start(), calls=%async_computation.3 | async-start | bytes 2129920 | tf_op jit(solution)/shard_map/all_gather | solution.py:97
  8.7 283.4 %all-gather.11.cloned.1.call-start = ((), (), s32[]{:S(2)}) async-start(), calls=%async_computation.4 | async-start | bytes 6291456 | tf_op jit(solution)/shard_map/all_gather | solution.py:32
  158.5 1.3 copy-start.2
  159.8 47.8 %collective-permute-start = (bf16[2048,512]{1,0:T(8,128)(2,1)S(1)}, bf16[2048,512]{1,0:T(8,128)(2,1)S(1)}, u32[]{:S(2)}, u32[]{:S(2)}) collective-permute-start(bf16[2048,512]{1,0:T(8,128)(2,1)S(1)} %fusion.16), channel_id=1, source_target_pairs={{0,64},{64,0},{1,65},{65,1},{2,66},{66,2},{3,67},{67,3},{4,68},{68... | collective-permute-start | bytes 6291464 | tf_op jit(solution)/shard_map/ppermute | solution.py:24
  207.6 1.4 copy-start.3
  235.8 140.0 %all-gather.13.cloned.1.call-start = ((), (), s32[]{:S(2)}) async-start(), calls=%async_computation.5 | async-start | bytes 6291456 | tf_op jit(solution)/shard_map/all_gather | solution.py:32
  297.1 83.6 %all-to-all-start = ((bf16[64,8,2048]{2,1,0:T(8,128)(2,1)}), bf16[64,8,2048]{2,1,0:T(8,128)(2,1)S(1)}, u32[]{:S(2)}, u32[]{:S(2)}) async-start(bf16[64,8,2048]{2,1,0:T(8,128)(2,1)} %bitcast.8), calls=%async_computation | async-start | bytes 4194304 | tf_op jit(solution)/shard_map/all_to_all | solution.py:42
  380.8 68.8 %all-to-all-start.1 = ((bf16[64,32,512]{2,1,0:T(8,128)(2,1)}), bf16[64,32,512]{2,1,0:T(8,128)(2,1)}, u32[]{:S(2)}, u32[]{:S(2)}) async-start(bf16[64,32,512]{2,1,0:T(8,128)(2,1)} %bitcast.10), calls=%async_computation.1 | async-start | bytes 4194304 | tf_op jit(solution)/shard_map/all_to_all | solution.py:42
Sparse Core Ops, SparseCore 0:
  11.2 70.6 all-gather.6
  84.9 65.0 all-gather.8
  235.9 56.1 all-gather.10
  293.6 82.1 all-gather.12
where the time goes:
time: 461 us; the launch traced here: 460 us
  waiting for transfers between devices  281 us (61%)
  matrix products  63.9 us (14%)
  blocking collectives  49.3 us (11%)
  other arithmetic  25.1 us (5%)
  starting transfers between devices  21.7 us (5%)
  between operations  15.7 us (3%)
    all_gather x2, waiting for transfers between devices, total_of_pieces(): return lax.all_gather(x, axis).astype(jnp.float32).sum(0)  111 us
    all_gather x1, waiting for transfers between devices, on_device(): lax.all_gather(w_in, FSDP, axis=0, tiled=True)  67.6 us
    all_gather x1, waiting for transfers between devices, on_device(): lax.all_gather(w_out, FSDP, axis=0, tiled=True)  54.5 us
    psum x5, blocking collectives, over_axes(): return functools.reduce(lax.psum, axes, x)  49.3 us
    ppermute x1, waiting for transfers between devices, swapped(): return lax.ppermute(block, axis, route)  47.2 us
    dot_general x1, matrix products, on_device(): lax.dot_general(normed, dpre, contract, preferred_element_type=jnp.float32)  26.8 us
    all_to_all x2, starting transfers between devices, sum_at_owner(): tiles = lax.all_to_all(in_blocks(x, dim, count), axis, 0, 0, tiled=True)  20.8 us
    dot_general x1, matrix products, on_device(): lax.dot_general(act, dpred, contract, preferred_element_type=jnp.float32)  13.9 us
  transfers between devices with their start and end apart: 7, of which 5 were waited for; matrix products, arithmetic and copies ran while one was open for 11% of the time, Pallas kernels for 0%

commit v1 on v0

v1 whole, which is shorter than its diff:
```python
import jax
import jax.numpy as jnp
from jax import lax
from jax.experimental import pallas as pl
from jax.experimental.pallas import tpu as pltpu
from jax.sharding import Mesh
from jax.sharding import PartitionSpec as P

M, Z, Y, X, C = AXES = ("member", "fsdp_0", "fsdp_1", "fsdp_2", "fsdp_3")
FSDP = (Z, Y, X, C)
MESH = pl.DeviceIdType.MESH
F32 = jnp.float32
BF16 = jnp.bfloat16

COEF = 0.7978845608
CUBIC = 0.044715

D = 512
H = 2048
ROWS = 2048
HALF = 1024
NODES = 131072
TILE = 256
TILES = HALF // TILE


def remote(src, dst, send, recv, device):
    return pltpu.make_async_remote_copy(
        src_ref=src, dst_ref=dst, send_sem=send, recv_sem=recv, device_id=device, device_id_type=MESH
    )


def dot(a, b):
    return jnp.dot(a, b, preferred_element_type=F32)


def dot_t(a, b):
    return lax.dot_general(a, b, (((1,), (1,)), ((), ())), preferred_element_type=F32)


def gain_of(noise, cond):
    n = noise.shape[1]
    square = (n, n)
    same = lax.broadcasted_iota(jnp.int32, square, 0) == lax.broadcasted_iota(jnp.int32, square, 1)
    column = jnp.sum(jnp.where(same, jnp.broadcast_to(noise, square), 0.0), axis=1, keepdims=True)
    return jnp.sum(column * cond, axis=0, keepdims=True)


def kernel(
    latents, noise, cond_gain, cond_shift, w_in, b_in, w_out, target,
    out, g_in, g_out, loss,
    wi, wo, lat, tgt, pbuf, nrm, nt, dp, dt, act, slp, nz,
    si, so, ri, ro, ihr, ihq, ifr, ifq, ohr, ohq, ofr, ofq,
    ic, oc, jhr, jhq, jfr, jfq, phr, phq, pfr, pfq,
    xi, xir, xo, xor, yi, yir, yo, yor, cr, crr,
    s_ld, s_out, s_lat, r_lat, s_prd, r_prd, s_nz, r_nz,
    s_w0, r_w0, l_w0, s_ag, r_ag, s_sib, r_sib, s_core, r_core, s_rs, r_rs, s_x, r_x, s_cr, r_cr,
):
    m, z, y, h, c = [lax.axis_index(a) for a in AXES]
    up = {Y: {Y: lax.rem(y + 1, 4)}, Z: {Z: lax.rem(z + 1, 4)}}
    down = {Y: {Y: lax.rem(y + 3, 4)}, Z: {Z: lax.rem(z + 3, 4)}}
    place = {Y: y, Z: z}
    sib = {C: 1 - c}
    pair = {M: 1 - m}
    near = {X: 1 - h, M: 1 - m}
    cross = {X: 1 - h, M: 1 - m, C: 1 - c}

    mine, theirs = m * HALF, (1 - m) * HALF

    def load_own(t):
        return pltpu.make_async_copy(
            latents.at[0, pl.ds(mine + t * TILE, TILE)], lat.at[0, pl.ds(t * TILE, TILE)], s_ld.at[t]
        )

    load_target = pltpu.make_async_copy(target.at[pl.ds(mine, HALF)], tgt, s_ld.at[TILES])
    for t in range(TILES):
        load_own(t).start()
    load_target.start()

    barrier = pltpu.get_barrier_semaphore()
    greeted = [sib, pair, near, cross, up[Y], down[Y], up[Z], down[Z]]
    for other in greeted:
        pl.semaphore_signal(barrier, inc=1, device_id=other, device_id_type=MESH)
    pl.semaphore_wait(barrier, len(greeted))

    def shard_parts(h_from, c_from, c_to):
        row = 2 * h_from + c_from
        parts = []
        for k in range(2):
            col = pl.ds(pl.multiple_of(c_to * 1024 + k * 512, 512), 512)
            parts.append((w_in.at[:, col], wi.at[2 * c_to + k, z, y, pl.ds(8 * row, 8)]))
        for k in range(2):
            col = pl.ds(pl.multiple_of(c_to * 256 + k * 128, 128), 128)
            parts.append((w_out.at[:, col], wo.at[2 * c_to + k, z, y, pl.ds(32 * row, 32)]))
        return parts

    partners = [(near, 1 - h, c), (cross, 1 - h, 1 - c), (sib, h, 1 - c)]
    first_sends = []
    for n, (src, dst) in enumerate(shard_parts(h, c, c)):
        pltpu.make_async_copy(src, dst, l_w0.at[n]).start()
    for n in range(4):
        for r, (who, _, c_to) in enumerate(partners):
            src, dst = shard_parts(h, c, c_to)[n]
            copy = remote(src, dst, s_w0.at[r, n], r_w0.at[r, n], who)
            copy.start()
            first_sends.append(copy)

    noise_copy = remote(noise, nz, s_nz, r_nz, pair)
    noise_copy.start()

    def send_latents(t):
        return remote(
            latents.at[0, pl.ds(theirs + t * TILE, TILE)],
            lat.at[1, pl.ds(t * TILE, TILE)],
            s_lat.at[t],
            r_lat.at[t],
            pair,
        )

    for t in range(TILES):
        send_latents(t).start()

    streams = [(wi, 0, Y), (wi, 1, Z), (wo, 0, Y), (wo, 1, Z)]

    def other_axis(a):
        return Z if a == Y else Y

    def gather_view(s, phase, i, part):
        ref, k, first = streams[s]
        size = ref.shape[3]
        rows = pl.ds(0, size) if part is None else pl.ds(part * size // 2, size // 2)
        block = 2 * c + k
        if phase == 0:
            return ref.at[block, z, i, rows] if first == Y else ref.at[block, i, y, rows]
        return ref.at[block, i, :, rows] if first == Y else ref.at[block, :, i, rows]

    def gather_copy(s, phase, n):
        axis = streams[s][2] if phase == 0 else other_axis(streams[s][2])
        p = place[axis]
        i = [p, p, lax.rem(p + 3, 4), lax.rem(p + 1, 4)][n]
        view = gather_view(s, phase, i, [None, None, 0, 1][n])
        who = [up, down, up, down][n][axis]
        return remote(view, view, s_ag.at[s, phase, n], r_ag.at[s, phase, n], who)

    def gather_landed(s, phase, n):
        axis = streams[s][2] if phase == 0 else other_axis(streams[s][2])
        p = place[axis]
        i = lax.rem(p + [3, 1, 2, 2][n], 4)
        view = gather_view(s, phase, i, [None, None, 0, 1][n])
        remote(view, view, s_ag.at[s, phase, n], r_ag.at[s, phase, n], up[axis]).wait_recv()

    def gather_start(s, phase):
        gather_copy(s, phase, 0).start()
        gather_copy(s, phase, 1).start()

    def gather_forward(s, phase):
        gather_landed(s, phase, 0)
        gather_copy(s, phase, 2).start()
        gather_landed(s, phase, 1)
        gather_copy(s, phase, 3).start()

    def gather_end(s, phase):
        gather_landed(s, phase, 2)
        gather_landed(s, phase, 3)
        for n in range(4):
            gather_copy(s, phase, n).wait_send()

    def share(s, block_of):
        ref, k, _ = streams[s]
        view = ref.at[2 * block_of + k]
        return remote(view, view, s_sib.at[s], r_sib.at[s], sib)

    for n in range(4):
        src, dst = shard_parts(h, c, c)[n]
        pltpu.make_async_copy(src, dst, l_w0.at[n]).wait()
        for r, (who, h_from, c_from) in enumerate(partners):
            src, dst = shard_parts(h_from, c_from, c)[n]
            remote(src, dst, s_w0.at[r, n], r_w0.at[r, n], who).wait_recv()
        gather_start(n, 0)
    for copy in first_sends:
        copy.wait_send()
    for s in range(4):
        gather_forward(s, 0)
    for s in range(4):
        gather_end(s, 0)
        gather_start(s, 1)
    for s in range(4):
        gather_forward(s, 1)
    for s in range(4):
        gather_end(s, 1)
        share(s, c).start()

    noise_copy.wait()
    gains = [1.0 + gain_of(noise[...], cond_gain[...]), 1.0 + gain_of(nz[...], cond_gain[...])]
    shifts = [gain_of(noise[...], cond_shift[...]), gain_of(nz[...], cond_shift[...])]

    for s in range(4):
        share(s, c).wait_send()
        share(s, 1 - c).wait_recv()

    def w_out_rows(j):
        return jnp.concatenate([wo[b, j].reshape(512, 128) for b in range(4)], axis=1)

    def forward(slot, t):
        row = pl.multiple_of(slot * HALF + t * TILE, TILE)
        rows = pl.ds(row, TILE)
        x = lat[slot, pl.ds(pl.multiple_of(t * TILE, TILE), TILE), :].astype(F32)
        centred = x - jnp.mean(x, axis=1, keepdims=True)
        spread = jnp.mean(centred * centred, axis=1, keepdims=True)
        normed = centred * lax.rsqrt(spread + 0.25) * gains[slot] + shifts[slot]
        nrm[...] = normed.astype(BF16)
        nt[:, rows] = normed.T.astype(BF16)

        def hidden(j, carry):
            v = dot(nrm[...], wi[j].reshape(512, 512)) + b_in[pl.ds(j, 1), :]
            q = v * v
            u = jnp.tanh(v * (COEF + (COEF * CUBIC) * q))
            half = 0.5 + 0.5 * u
            a = v * half
            slope = half + a * ((1.0 - half) * (2.0 * COEF + (6.0 * COEF * CUBIC) * q))
            act[j, rows, :] = a.astype(BF16)
            slp[j, rows, :] = slope.astype(BF16)
            return carry

        lax.fori_loop(0, 4, hidden, 0)
        for j in range(4):
            x = x + dot(act[j, rows, :], w_out_rows(j))
        pbuf[slot, pl.ds(pl.multiple_of(t * TILE, TILE), TILE), :] = x.astype(BF16)

    def store_own(t):
        return pltpu.make_async_copy(
            pbuf.at[0, pl.ds(t * TILE, TILE)], out.at[0, pl.ds(mine + t * TILE, TILE)], s_out.at[t]
        )

    def send_prediction(t):
        return remote(
            pbuf.at[1, pl.ds(t * TILE, TILE)],
            out.at[0, pl.ds(mine + t * TILE, TILE)],
            s_prd.at[t],
            r_prd.at[t],
            pair,
        )

    def own_tile(t, carry):
        load_own(t).wait()
        forward(0, t)
        store_own(t).start()
        return carry

    lax.fori_loop(0, TILES, own_tile, 0)

    load_target.wait()
    cr[0] = jnp.zeros((8, 128), F32)
    scale = float((2 * NODES) ** -0.5)

    def both_tile(t, carry):
        send_latents(t).wait_recv()
        forward(1, t)
        send_prediction(t).start()
        rows = pl.ds(pl.multiple_of(t * TILE, TILE), TILE)
        p0 = pbuf[0, rows, :].astype(F32)
        p1 = pbuf[1, rows, :].astype(F32)
        goal = tgt[rows, :].astype(F32)
        near0, near1, apart = p0 - goal, p1 - goal, p0 - p1
        q0, q1, qa = near0 * near0 + 0.0625, near1 * near1 + 0.0625, apart * apart + 0.0625
        i0, i1, ia = lax.rsqrt(q0), lax.rsqrt(q1), lax.rsqrt(qa)
        crps = 0.5 * (q0 * i0 + q1 * i1 - qa * ia)
        summed = jnp.sum(crps.reshape(TILE // 8, 8, D), axis=0)
        cr[0] += sum(summed[:, k * 128 : (k + 1) * 128] for k in range(4))
        pull = 0.5 * apart * ia
        grads = ((0.5 * near0 * i0 - pull) * scale, (0.5 * near1 * i1 + pull) * scale)
        for slot in range(2):
            dp[slot] = grads[slot].astype(BF16)
            dt[:, pl.ds(pl.multiple_of(slot * HALF + t * TILE, TILE), TILE)] = grads[slot].T.astype(BF16)

        def hidden(j, carry):
            w = w_out_rows(j)
            for slot in range(2):
                at = pl.ds(pl.multiple_of(slot * HALF + t * TILE, TILE), TILE)
                slp[j, at, :] = (dot_t(dp[slot], w) * slp[j, at, :].astype(F32)).astype(BF16)
            return carry

        lax.fori_loop(0, 4, hidden, 0)
        return carry

    lax.fori_loop(0, TILES, both_tile, 0)

    def core_copy(n, j, half):
        if n == 0:
            k = 2 * j + half
            return remote(si.at[1 - c, k], ri.at[k], s_core.at[0, k], r_core.at[0, k], sib)
        ys = pl.ds(2 * half, 2)
        k = 2 * j + half
        return remote(so.at[1 - c, j, ys], ro.at[j, ys], s_core.at[1, k], r_core.at[1, k], sib)

    def grads_of(j, carry):
        for half in range(2):
            cols = slice(256 * half, 256 * half + 256)
            gi = dot(nt[...], slp[j, :, cols]).reshape(32, 2, 8, 256)
            go = dot(dt[...], act[j, :, cols]).T.reshape(2, 2, 2, 32, 512)
            for core in range(2):
                si[core, 2 * j + half] = gi[:, core].reshape(4, 4, 16, 256).astype(BF16)
                so[core, j, 2 * half : 2 * half + 2] = go[:, :, core].reshape(2, 64, 512).astype(BF16)
            core_copy(0, j, half).start()
            core_copy(1, j, half).start()
        return carry

    lax.fori_loop(0, 4, grads_of, 0)

    def add_sibling(j, carry):
        for half in range(2):
            k = 2 * j + half
            core_copy(0, j, half).wait()
            si[c, k] = (si[c, k].astype(F32) + ri[k].astype(F32)).astype(BF16)
            core_copy(1, j, half).wait()
            ys = pl.ds(2 * half, 2)
            so[c, j, ys] = (so[c, j, ys].astype(F32) + ro[j, ys].astype(F32)).astype(BF16)
        return carry

    lax.fori_loop(0, 4, add_sibling, 0)

    mates = [
        sib,
        near,
        pair,
        {Y: y + 1 - 2 * lax.rem(y, 2)},
        {Y: 3 - y},
        {Z: z + 1 - 2 * lax.rem(z, 2)},
        {Z: 3 - z},
    ]

    def loss_copy(n):
        return remote(cr.at[n], crr.at[n], s_cr.at[n], r_cr.at[n], mates[n])

    def loss_next(n):
        loss_copy(n).wait()
        cr[n + 1] = cr[n] + crr[n]
        if n + 1 < len(mates):
            loss_copy(n + 1).start()

    loss_copy(0).start()

    def i_first(i, part):
        return si.at[c, pl.ds(4 * part, 4), :, i]

    def o_first(i, part):
        return so.at[c, i, :, pl.ds(32 * part, 32)]

    def i_second(i, part):
        return ic.at[pl.ds(4 * part, 4), i]

    def o_second(i, part):
        return oc.at[i, pl.ds(32 * part, 32)]

    def ring_sums(n, axis, view, hr, hq, fr, fq):
        p = place[axis]
        q, r, o = lax.rem(p + 1, 4), lax.rem(p + 3, 4), lax.rem(p + 2, 4)

        def move(k):
            src, dst, who = [
                (view(o, 0), hr, up),
                (view(o, 1), hq, down),
                (view(q, 1), fr.at[1], up),
                (view(r, 0), fq.at[0], down),
                (view(q, 0), fr.at[0], up),
                (view(r, 1), fq.at[1], down),
            ][k]
            return remote(src, dst, s_rs.at[n, k], r_rs.at[n, k], who[axis])

        def begin():
            for k in range(4):
                move(k).start()

        def middle():
            for k, i, part, got in ((0, q, 0, hr), (1, r, 1, hq)):
                move(k).wait_recv()
                block = view(i, part)
                block[...] = (block[...].astype(F32) + got[...].astype(F32)).astype(BF16)
                move(4 + k).start()

        def end():
            for k in (2, 3, 4, 5):
                move(k).wait_recv()
            sums = []
            for part in range(2):
                sums.append(
                    view(p, part)[...].astype(F32) + (fr[part].astype(F32) + fq[part].astype(F32))
                )
            for k in range(6):
                move(k).wait_send()
            return sums

        return begin, middle, end

    i1 = ring_sums(0, Y, i_first, ihr, ihq, ifr, ifq)
    o1 = ring_sums(1, Z, o_first, ohr, ohq, ofr, ofq)
    i2 = ring_sums(2, Z, i_second, jhr, jhq, jfr, jfq)
    o2 = ring_sums(3, Y, o_second, phr, phq, pfr, pfq)
    i1[0]()
    o1[0]()
    loss_next(0)
    i1[1]()
    o1[1]()
    loss_next(1)
    for part, v in enumerate(i1[2]()):
        ic[4 * part : 4 * part + 4] = v.astype(BF16)
    i2[0]()
    for part, v in enumerate(o1[2]()):
        oc[:, 32 * part : 32 * part + 32] = v.astype(BF16)
    o2[0]()
    loss_next(2)
    i2[1]()
    o2[1]()
    loss_next(3)
    sum_i = jnp.concatenate(i2[2](), axis=0)
    xi[...] = jnp.where(h == 0, sum_i[:, 8:], sum_i[:, :8])
    i_copy = remote(xi, xir, s_x.at[0], r_x.at[0], near)
    i_copy.start()
    low, high = o2[2]()
    xo[...] = jnp.where(h == 0, high, low)
    o_copy = remote(xo, xor, s_x.at[1], r_x.at[1], near)
    o_copy.start()
    own_i = jnp.where(h == 0, sum_i[:, :8], sum_i[:, 8:])
    own_o = jnp.where(h == 0, low, high)
    loss_next(4)
    i_copy.wait()
    yi[...] = own_i + xir[...]
    i_copy = remote(yi, yir, s_x.at[2], r_x.at[2], pair)
    i_copy.start()
    o_copy.wait()
    yo[...] = own_o + xor[...]
    o_copy = remote(yo, yor, s_x.at[3], r_x.at[3], pair)
    o_copy.start()
    loss_next(5)
    i_copy.wait()
    for k in range(8):
        g_in[:, 256 * k : 256 * k + 256] = yi[k] + yir[k]
    o_copy.wait()
    g_out[...] = yo[...] + yor[...]
    loss_next(6)
    loss[0, 0] = jnp.sum(cr[7]) / float(2 * NODES * D)

    for t in range(TILES):
        store_own(t).wait()
        send_latents(t).wait_send()
        send_prediction(t).wait_send()
        remote(
            pbuf.at[1, pl.ds(t * TILE, TILE)],
            out.at[0, pl.ds(theirs + t * TILE, TILE)],
            s_prd.at[t],
            r_prd.at[t],
            pair,
        ).wait_recv()


def vm(*shape, dtype=BF16):
    return pltpu.VMEM(shape, dtype)


def dma(*shape):
    return pltpu.SemaphoreType.DMA(shape)


SCRATCH = [
    vm(4, 4, 4, 32, 512), vm(4, 4, 4, 128, 128), vm(2, HALF, D), vm(HALF, D), vm(2, HALF, D),
    vm(TILE, D), vm(D, ROWS), vm(2, TILE, D), vm(D, ROWS), vm(4, ROWS, 512), vm(4, ROWS, 512), vm(1, 32, dtype=F32),
    vm(2, 8, 4, 4, 16, 256), vm(2, 4, 4, 64, 512), vm(8, 4, 4, 16, 256), vm(4, 4, 64, 512),
    vm(4, 4, 16, 256), vm(4, 4, 16, 256), vm(2, 4, 4, 16, 256), vm(2, 4, 4, 16, 256),
    vm(4, 32, 512), vm(4, 32, 512), vm(2, 4, 32, 512), vm(2, 4, 32, 512),
    vm(8, 4, 16, 256), vm(4, 64, 512),
    vm(4, 16, 256), vm(4, 16, 256), vm(2, 4, 16, 256), vm(2, 4, 16, 256),
    vm(32, 512), vm(32, 512), vm(2, 32, 512), vm(2, 32, 512),
    vm(8, 8, 256, dtype=F32), vm(8, 8, 256, dtype=F32), vm(32, 512, dtype=F32), vm(32, 512, dtype=F32),
    vm(8, 8, 256, dtype=F32), vm(8, 8, 256, dtype=F32), vm(32, 512, dtype=F32), vm(32, 512, dtype=F32),
    vm(8, 8, 128, dtype=F32), vm(7, 8, 128, dtype=F32),
    dma(TILES + 1), dma(TILES), dma(TILES), dma(TILES), dma(TILES), dma(TILES),
    pltpu.SemaphoreType.DMA, pltpu.SemaphoreType.DMA,
    dma(3, 4), dma(3, 4), dma(4), dma(4, 2, 4), dma(4, 2, 4), dma(4), dma(4), dma(2, 8), dma(2, 8),
    dma(4, 6), dma(4, 6), dma(4), dma(4), dma(7), dma(7),
]


def on_device(latents, noise, cond_gain, cond_shift, w_in, b_in, w_out, target):
    inside = pl.BlockSpec(memory_space=pltpu.VMEM)
    anywhere = pl.BlockSpec(memory_space=pl.ANY)
    prediction, grad_in, grad_out, loss = pl.pallas_call(
        kernel,
        out_shape=(
            jax.ShapeDtypeStruct((1, ROWS, D), BF16),
            jax.ShapeDtypeStruct((8, H), F32),
            jax.ShapeDtypeStruct((32, D), F32),
            jax.ShapeDtypeStruct((1, 1), F32),
        ),
        in_specs=[anywhere] + [inside] * 6 + [anywhere],
        out_specs=(anywhere, inside, inside, pl.BlockSpec(memory_space=pltpu.SMEM)),
        scratch_shapes=SCRATCH,
        compiler_params=pltpu.CompilerParams(
            collective_id=0, has_side_effects=True, vmem_limit_bytes=63 * 1024 * 1024
        ),
    )(latents, noise, cond_gain, cond_shift, w_in, b_in.reshape(4, 512), w_out, target)
    return prediction, grad_in, grad_out, loss.reshape(())


def solution(mesh):
    torus = Mesh(mesh.devices.reshape(2, 4, 4, 2, 2), AXES)
    in_specs = (
        P(M, FSDP, None),
        P(M, None),
        P(),
        P(),
        P(FSDP, None),
        P(),
        P(FSDP, None),
        P(FSDP, None),
    )
    out_specs = (P(M, FSDP, None), P(FSDP, None), P(FSDP, None), P())
    return jax.shard_map(on_device, mesh=torus, in_specs=in_specs, out_specs=out_specs, check_vma=False)
```

time: 461 us -> 116 us (0.25)
  waiting for transfers between devices: 281 us -> 0 us
  Pallas kernels: 0 us -> 108 us
  matrix products: 63.9 us -> 0 us
  blocking collectives: 49.3 us -> 0 us
  other arithmetic: 25.1 us -> 0 us
  starting transfers between devices: 21.7 us -> 0 us
  between operations: 15.7 us -> 2.46 us
    all_gather x4 -> x0, waiting for transfers between devices: 233 us -> none  [the longest x2 111 us: total_of_pieces(): return lax.all_gather(x, axis).astype(jnp.float32).sum(0)]
    pallas_call x0 -> x1, Pallas kernels: none -> 108 us  [on_device(): pl.pallas_call(kernel, out_shape=(jax.ShapeDtypeStruct((1, ROWS, D), BF16...]
    dot_general x6 -> x0, matrix products: 63.9 us -> none  [the longest x1 26.8 us: on_device(): lax.dot_general(normed, dpre, contract, preferred_element_type=jnp.float32)]
    psum x5 -> x0, blocking collectives: 49.3 us -> none  [over_axes(): return functools.reduce(lax.psum, axes, x)]
    ppermute x1 -> x0, waiting for transfers between devices: 47.2 us -> none  [swapped(): return lax.ppermute(block, axis, route)]
    reduce_sum x7 -> x0, other arithmetic: 25 us -> none  [the longest x2 10 us: total_of_pieces(): return lax.all_gather(x, axis).astype(jnp.float32).sum(0)]
    all_to_all x2 -> x0, starting transfers between devices: 20.8 us -> none  [sum_at_owner(): tiles = lax.all_to_all(in_blocks(x, dim, count), axis, 0, 0, tiled=True)]
  transfers between devices with their start and end apart: 7 -> 0, of which waited for: 5 -> 0; matrix products, arithmetic and copies ran while one was open for 11% -> 0% of each run, Pallas kernels for 0% -> 0%
where the time goes in v1:
time: 116 us
  Pallas kernels  108 us (93%)
  local copies, waits for them, and re-layouts  5.65 us (5%)
  between operations  2.46 us (2%)
    pallas_call x1, Pallas kernels, on_device(): pl.pallas_call(kernel, out_shape=(jax.ShapeDtypeStruct((1, ROWS, D), BF16...  108 us
    unnamed x7, local copies, waits for them, and re-layouts  4.35 us

profile of v1, /device:TPU:0, one launch (start us, length us, event | category | flops | bytes accessed | tf_op | source)
XLA Modules:
  0.0 116.2 jit_solution(8547869590247187604)
XLA Ops:
  0.6 1.3 %reshape.14.b_in = f32[4,512]{1,0:T(4,128)} reshape(f32[2048]{0:T(1024)} %param.13) | data formatting | bytes 16384 | tf_op jit(solution)/shard_map/reshape | solution.py:500
  1.9 108.1 %shard_map.111 = (bf16[1,2048,512]{2,1,0:T(8,128)(2,1)}, f32[8,2048]{1,0:T(8,128)}, f32[32,512]{1,0:T(8,128)}, f32[1,1]{1,0:T(1,128)}) custom-call(bf16[1,2048,512]{2,1,0:T(8,128)(2,1)} %latents.1, f32[1,32]{1,0:T(1,128)} %noise.1, f32[32,512]{1,0:T(8,128)} %cond_gain.1, f32[32,512]{1,0:T(8,128)} %cond_shift.1, bf16[8,2048]{1,0:T(8,128)(2,1)} %w_in.1, ...), custom_call_target="tpu_custom_call" | custom-call | tf_op jit(solution)/shard_map/pallas_call | solution.py:486
  110.0 0.0 copy-start.1
  110.0 0.0 copy-start
  110.1 3.1 %copy.16 = bf16[1,2048,512]{2,1,0:T(8,128)(2,1)} copy(bf16[1,2048,512]{2,1,0:T(8,128)(2,1)} %get-tuple-element.16) | data formatting | bytes 4194304
  113.1 0.0 copy-done.1
  113.1 0.6 copy.17
  113.8 0.0 copy-done
  113.8 0.6 copy.18
Async XLA Ops:
  110.0 3.1 %copy-start.1 = (f32[8,2048]{1,0:T(8,128)S(1)}, f32[8,2048]{1,0:T(8,128)}, u32[]{:S(2)}) copy-start(f32[8,2048]{1,0:T(8,128)} %get-tuple-element.17) | copy-start | bytes 196612
  110.0 3.7 %copy-start = (f32[32,512]{1,0:T(8,128)S(1)}, f32[32,512]{1,0:T(8,128)}, u32[]{:S(2)}) copy-start(f32[32,512]{1,0:T(8,128)} %get-tuple-element.18) | copy-start | bytes 196612

commit v2 on v1

v2 whole, which is shorter than its diff:
```python
import functools

import jax
import jax.numpy as jnp
from jax import lax
from jax.experimental import pallas as pl
from jax.experimental.pallas import tpu as pltpu
from jax.sharding import Mesh
from jax.sharding import PartitionSpec as P

M, Z, Y, X, C = AXES = ("member", "fsdp_0", "fsdp_1", "fsdp_2", "fsdp_3")
FSDP = (Z, Y, X, C)
MESH = pl.DeviceIdType.MESH
F32 = jnp.float32
BF16 = jnp.bfloat16

COEF = 0.7978845608
CUBIC = 0.044715

D = 512
H = 2048
ROWS = 2048
HALF = 1024
NODES = 131072
TILE = 256
TILES = HALF // TILE


def remote(src, dst, send, recv, device):
    return pltpu.make_async_remote_copy(
        src_ref=src, dst_ref=dst, send_sem=send, recv_sem=recv, device_id=device, device_id_type=MESH
    )


def dot(a, b):
    return jnp.dot(a, b, preferred_element_type=F32)


def dot_t(a, b):
    return lax.dot_general(a, b, (((1,), (1,)), ((), ())), preferred_element_type=F32)


def gain_of(noise, cond):
    n = noise.shape[1]
    square = (n, n)
    same = lax.broadcasted_iota(jnp.int32, square, 0) == lax.broadcasted_iota(jnp.int32, square, 1)
    column = jnp.sum(jnp.where(same, jnp.broadcast_to(noise, square), 0.0), axis=1, keepdims=True)
    return jnp.sum(column * cond, axis=0, keepdims=True)


def kernel(
    latents, noise, cond_gain, cond_shift, w_in, b_in, w_out, target,
    out, g_in, g_out, loss,
    wi, wo, lat, tgt, pbuf, nrm, nt, dp, dt, act, slp, nz,
    si, so, ri, ro, ihr, ihq, ifr, ifq, ohr, ohq, ofr, ofq,
    ic, oc, jhr, jhq, jfr, jfq, phr, phq, pfr, pfq,
    xi, xir, xo, xor, cr, crr,
    s_ld, s_out, s_lat, r_lat, s_prd, r_prd, s_nz, r_nz,
    s_w0, r_w0, l_w0, s_ag, r_ag, s_sib, r_sib, s_core, r_core, s_rs, r_rs, s_x, r_x, s_cr, r_cr,
):
    m, z, y, h, c = [lax.axis_index(a) for a in AXES]
    up = {Y: {Y: lax.rem(y + 1, 4)}, Z: {Z: lax.rem(z + 1, 4)}}
    down = {Y: {Y: lax.rem(y + 3, 4)}, Z: {Z: lax.rem(z + 3, 4)}}
    place = {Y: y, Z: z}
    sib = {C: 1 - c}
    pair = {M: 1 - m}
    near = {X: 1 - h, M: 1 - m}
    cross = {X: 1 - h, M: 1 - m, C: 1 - c}

    mine, theirs = m * HALF, (1 - m) * HALF

    def load_own(t):
        return pltpu.make_async_copy(
            latents.at[0, pl.ds(mine + t * TILE, TILE)], lat.at[0, pl.ds(t * TILE, TILE)], s_ld.at[t]
        )

    load_target = pltpu.make_async_copy(target.at[pl.ds(mine, HALF)], tgt, s_ld.at[TILES])
    for t in range(TILES):
        load_own(t).start()
    load_target.start()

    barrier = pltpu.get_barrier_semaphore()
    greeted = [sib, pair, near, cross, {X: 1 - h}, up[Y], down[Y], up[Z], down[Z]]
    for other in greeted:
        pl.semaphore_signal(barrier, inc=1, device_id=other, device_id_type=MESH)
    pl.semaphore_wait(barrier, len(greeted))

    def shard_parts(h_from, c_from, c_to):
        row = 2 * h_from + c_from
        parts = []
        for k in range(2):
            col = pl.ds(pl.multiple_of(c_to * 1024 + k * 512, 512), 512)
            parts.append((w_in.at[:, col], wi.at[2 * c_to + k, z, y, pl.ds(8 * row, 8)]))
        for k in range(2):
            col = pl.ds(pl.multiple_of(c_to * 256 + k * 128, 128), 128)
            parts.append((w_out.at[:, col], wo.at[2 * c_to + k, z, y, pl.ds(32 * row, 32)]))
        return parts

    partners = [(near, 1 - h, c), (cross, 1 - h, 1 - c), (sib, h, 1 - c)]
    first_sends = []
    for n, (src, dst) in enumerate(shard_parts(h, c, c)):
        pltpu.make_async_copy(src, dst, l_w0.at[n]).start()
    for n in range(4):
        for r, (who, _, c_to) in enumerate(partners):
            src, dst = shard_parts(h, c, c_to)[n]
            copy = remote(src, dst, s_w0.at[r, n], r_w0.at[r, n], who)
            copy.start()
            first_sends.append(copy)

    noise_copy = remote(noise, nz, s_nz, r_nz, pair)
    noise_copy.start()

    def send_latents(t):
        return remote(
            latents.at[0, pl.ds(theirs + t * TILE, TILE)],
            lat.at[1, pl.ds(t * TILE, TILE)],
            s_lat.at[t],
            r_lat.at[t],
            pair,
        )

    for t in range(TILES):
        send_latents(t).start()

    def tile_of(slot, t):
        return pl.ds(pl.multiple_of(slot * HALF + t * TILE, TILE), TILE)

    def normalise(slot, t, gain, shift):
        if slot == 0:
            load_own(t).wait()
        else:
            send_latents(t).wait_recv()
        x = lat[slot, tile_of(0, t), :].astype(F32)
        centred = x - jnp.mean(x, axis=1, keepdims=True)
        spread = jnp.mean(centred * centred, axis=1, keepdims=True)
        normed = centred * lax.rsqrt(spread + 0.25) * gain + shift
        nt[:, tile_of(slot, t)] = normed.T.astype(BF16)
        nrm[slot, tile_of(0, t), :] = normed.astype(BF16)

    gain, shift = 1.0 + gain_of(noise[...], cond_gain[...]), gain_of(noise[...], cond_shift[...])
    for t in range(2):
        normalise(0, t, gain, shift)
    streams = [(wi, 0, Y), (wi, 1, Z), (wo, 0, Y), (wo, 1, Z)]

    def other_axis(a):
        return Z if a == Y else Y

    def gather_view(s, phase, i, part):
        ref, k, first = streams[s]
        size = ref.shape[3]
        rows = pl.ds(0, size) if part is None else pl.ds(part * size // 2, size // 2)
        block = 2 * c + k
        if phase == 0:
            return ref.at[block, z, i, rows] if first == Y else ref.at[block, i, y, rows]
        return ref.at[block, i, :, rows] if first == Y else ref.at[block, :, i, rows]

    def gather_copy(s, phase, n):
        axis = streams[s][2] if phase == 0 else other_axis(streams[s][2])
        p = place[axis]
        i = [p, p, lax.rem(p + 3, 4), lax.rem(p + 1, 4)][n]
        view = gather_view(s, phase, i, [None, None, 0, 1][n])
        who = [up, down, up, down][n][axis]
        return remote(view, view, s_ag.at[s, phase, n], r_ag.at[s, phase, n], who)

    def gather_landed(s, phase, n):
        axis = streams[s][2] if phase == 0 else other_axis(streams[s][2])
        p = place[axis]
        i = lax.rem(p + [3, 1, 2, 2][n], 4)
        view = gather_view(s, phase, i, [None, None, 0, 1][n])
        remote(view, view, s_ag.at[s, phase, n], r_ag.at[s, phase, n], up[axis]).wait_recv()

    def gather_start(s, phase):
        gather_copy(s, phase, 0).start()
        gather_copy(s, phase, 1).start()

    def gather_forward(s, phase):
        gather_landed(s, phase, 0)
        gather_copy(s, phase, 2).start()
        gather_landed(s, phase, 1)
        gather_copy(s, phase, 3).start()

    def gather_end(s, phase):
        gather_landed(s, phase, 2)
        gather_landed(s, phase, 3)
        for n in range(4):
            gather_copy(s, phase, n).wait_send()

    def share(s, block_of):
        ref, k, _ = streams[s]
        view = ref.at[2 * block_of + k]
        return remote(view, view, s_sib.at[s], r_sib.at[s], sib)

    for n in range(4):
        src, dst = shard_parts(h, c, c)[n]
        pltpu.make_async_copy(src, dst, l_w0.at[n]).wait()
        for r, (who, h_from, c_from) in enumerate(partners):
            src, dst = shard_parts(h_from, c_from, c)[n]
            remote(src, dst, s_w0.at[r, n], r_w0.at[r, n], who).wait_recv()
        gather_start(n, 0)
    normalise(0, 2, gain, shift)
    for s in range(4):
        gather_forward(s, 0)
    normalise(0, 3, gain, shift)
    for s in range(2):
        gather_end(s, 0)
        gather_start(s, 1)
    noise_copy.wait()
    other_gain, other_shift = 1.0 + gain_of(nz[...], cond_gain[...]), gain_of(nz[...], cond_shift[...])
    normalise(1, 0, other_gain, other_shift)
    for s in range(2):
        gather_forward(s, 1)
    for s in range(2, 4):
        gather_end(s, 0)
        gather_start(s, 1)
    normalise(1, 1, other_gain, other_shift)
    for s in range(2):
        gather_end(s, 1)
        share(s, c).start()
    for s in range(2):
        share(s, 1 - c).wait_recv()

    def w_out_rows(j):
        return jnp.concatenate([wo[b, j].reshape(512, 128) for b in range(4)], axis=1)

    def hidden(j, slot, t):
        rows = tile_of(slot, t)
        v = dot(nrm[slot, tile_of(0, t), :], wi[j].reshape(512, 512)) + b_in[:, 512 * j : 512 * j + 512]
        q = v * v
        u = jnp.tanh(v * (COEF + (COEF * CUBIC) * q))
        half = 0.5 + 0.5 * u
        a = v * half
        slope = half + a * ((1.0 - half) * (2.0 * COEF + (6.0 * COEF * CUBIC) * q))
        a = a.astype(BF16)
        act[j, rows, :] = a
        slp[j, rows, :] = slope.astype(BF16)
        return a

    def store_own(t):
        return pltpu.make_async_copy(
            pbuf.at[0, pl.ds(t * TILE, TILE)], out.at[0, pl.ds(mine + t * TILE, TILE)], s_out.at[t]
        )

    def send_prediction(t):
        return remote(
            pbuf.at[1, pl.ds(t * TILE, TILE)],
            out.at[0, pl.ds(mine + t * TILE, TILE)],
            s_prd.at[t],
            r_prd.at[t],
            pair,
        )

    def own_hidden(t, carry):
        for j in range(4):
            hidden(j, 0, t)
        return carry

    def partner_hidden(t, carry):
        for j in range(4):
            hidden(j, 1, t)
        return carry

    def own_out(t, carry):
        x = lat[0, tile_of(0, t), :].astype(F32)
        for j in range(4):
            x = x + dot(act[j, tile_of(0, t), :], w_out_rows(j))
        pbuf[0, tile_of(0, t), :] = x.astype(BF16)
        store_own(t).start()
        return carry

    lax.fori_loop(0, 2, own_hidden, 0)
    for s in range(2, 4):
        gather_forward(s, 1)
    normalise(1, 2, other_gain, other_shift)
    lax.fori_loop(2, TILES, own_hidden, 0)
    normalise(1, 3, other_gain, other_shift)
    lax.fori_loop(0, 2, partner_hidden, 0)
    for s in range(2, 4):
        gather_end(s, 1)
        share(s, c).start()
    for s in range(2, 4):
        share(s, 1 - c).wait_recv()
    lax.fori_loop(0, TILES, own_out, 0)

    load_target.wait()
    cr[0] = jnp.zeros((8, 128), F32)
    scale = float((2 * NODES) ** -0.5)

    def both_tile(ready, t, carry):
        x = lat[1, tile_of(0, t), :].astype(F32)
        for j in range(4):
            a = act[j, tile_of(1, t), :] if ready else hidden(j, 1, t)
            x = x + dot(a, w_out_rows(j))
        pbuf[1, tile_of(0, t), :] = x.astype(BF16)
        send_prediction(t).start()
        rows = tile_of(0, t)
        p0 = pbuf[0, rows, :].astype(F32)
        p1 = x.astype(BF16).astype(F32)
        goal = tgt[rows, :].astype(F32)
        near0, near1, apart = p0 - goal, p1 - goal, p0 - p1
        q0, q1, qa = near0 * near0 + 0.0625, near1 * near1 + 0.0625, apart * apart + 0.0625
        i0, i1, ia = lax.rsqrt(q0), lax.rsqrt(q1), lax.rsqrt(qa)
        crps = q0 * i0 + q1 * i1 - qa * ia
        summed = jnp.sum(crps.reshape(TILE // 8, 8, D), axis=0)
        cr[0] += sum(summed[:, k * 128 : (k + 1) * 128] for k in range(4))
        pull = (0.5 * scale) * (apart * ia)
        grads = ((0.5 * scale) * (near0 * i0) - pull, (0.5 * scale) * (near1 * i1) + pull)
        for slot in range(2):
            dp[slot] = grads[slot].astype(BF16)
            dt[:, tile_of(slot, t)] = grads[slot].T.astype(BF16)
        for j in range(4):
            w = w_out_rows(j)
            for slot in range(2):
                at = tile_of(slot, t)
                slp[j, at, :] = (dot_t(dp[slot], w) * slp[j, at, :].astype(F32)).astype(BF16)
        return carry

    lax.fori_loop(0, 2, functools.partial(both_tile, True), 0)
    lax.fori_loop(2, TILES, functools.partial(both_tile, False), 0)

    mates = [
        sib,
        near,
        pair,
        {Y: y + 1 - 2 * lax.rem(y, 2)},
        {Y: 3 - y},
        {Z: z + 1 - 2 * lax.rem(z, 2)},
        {Z: 3 - z},
    ]

    def loss_copy(n):
        return remote(cr.at[n], crr.at[n], s_cr.at[n], r_cr.at[n], mates[n])

    def loss_next(n):
        loss_copy(n).wait()
        cr[n + 1] = cr[n] + crr[n]
        if n + 1 < len(mates):
            loss_copy(n + 1).start()

    blocks = [lax.rem(z + 2, 4), lax.rem(z + 1, 4), lax.rem(z + 3, 4), z]

    def core_copy(n, s, half):
        j, k = blocks[s], 2 * s + half
        if n == 0:
            at = 2 * j + half
            return remote(si.at[1 - c, at], ri.at[at], s_core.at[0, k], r_core.at[0, k], sib)
        ys = pl.ds(2 * half, 2)
        return remote(so.at[1 - c, j, ys], ro.at[j, ys], s_core.at[1, k], r_core.at[1, k], sib)

    def i_block(s):
        j = blocks[s]
        gi = dot(nt[...], slp[j]).reshape(32, 2, 8, 512)
        for half in range(2):
            for core in range(2):
                part = gi[:, core, :, 256 * half : 256 * half + 256]
                si[core, 2 * j + half] = part.reshape(4, 4, 16, 256).astype(BF16)
        for half in range(2):
            core_copy(0, s, half).start()

    def o_block(s):
        j = blocks[s]
        go = dot(dt[...], act[j]).T.reshape(4, 2, 2, 32, 512)
        for core in range(2):
            so[core, j] = go[:, :, core].reshape(4, 64, 512).astype(BF16)
        for half in range(2):
            core_copy(1, s, half).start()

    def i_add(s):
        for half in range(2):
            core_copy(0, s, half).wait_recv()
            k = 2 * blocks[s] + half
            si[c, k] = (si[c, k].astype(F32) + ri[k].astype(F32)).astype(BF16)

    def o_add(s):
        j = blocks[s]
        for half in range(2):
            core_copy(1, s, half).wait_recv()
            ys = pl.ds(2 * half, 2)
            so[c, j, ys] = (so[c, j, ys].astype(F32) + ro[j, ys].astype(F32)).astype(BF16)

    class Ring:
        def __init__(self, n, axis, view, hr, hq, fr, fq):
            p = place[axis]
            q, r, o = lax.rem(p + 1, 4), lax.rem(p + 3, 4), lax.rem(p + 2, 4)
            self.n, self.axis, self.view, self.p, self.q, self.r = n, axis, view, p, q, r
            self.hr, self.hq, self.fr, self.fq = hr, hq, fr, fq
            self.moves = [
                (view(o, 0), hr, up),
                (view(o, 1), hq, down),
                (view(q, 1), fr.at[1], up),
                (view(r, 0), fq.at[0], down),
                (view(q, 0), fr.at[0], up),
                (view(r, 1), fq.at[1], down),
            ]

        def move(self, k):
            src, dst, who = self.moves[k]
            return remote(src, dst, s_rs.at[self.n, k], r_rs.at[self.n, k], who[self.axis])

        def start(self, *ks):
            for k in ks:
                self.move(k).start()

        def relay(self, k):
            i, part, got = [(self.q, 0, self.hr), (self.r, 1, self.hq)][k]
            self.move(k).wait_recv()
            block = self.view(i, part)
            block[...] = (block[...].astype(F32) + got[...].astype(F32)).astype(BF16)
            self.move(4 + k).start()

        def begin(self):
            self.start(0, 1, 2, 3)

        def middle(self):
            self.relay(0)
            self.relay(1)

        def end(self):
            for k in (2, 3, 4, 5):
                self.move(k).wait_recv()
            return [
                self.view(self.p, part)[...].astype(F32)
                + (self.fr[part].astype(F32) + self.fq[part].astype(F32))
                for part in range(2)
            ]

        def drain(self):
            for k in range(6):
                self.move(k).wait_send()

    def i_ring(s):
        return Ring(
            s, Y, lambda i, part: si.at[c, 2 * blocks[s] + part, :, i],
            ihr.at[s], ihq.at[s], ifr.at[s], ifq.at[s],
        )

    i1 = [i_ring(s) for s in range(4)]
    i2 = Ring(4, Z, lambda i, part: ic.at[pl.ds(4 * part, 4), i], jhr, jhq, jfr, jfq)
    o1 = Ring(5, Z, lambda i, part: so.at[c, i, :, pl.ds(32 * part, 32)], ohr, ohq, ofr, ofq)
    o2 = Ring(6, Y, lambda i, part: oc.at[i, pl.ds(32 * part, 32)], phr, phq, pfr, pfq)

    def i_end(s):
        for part, v in enumerate(i1[s].end()):
            ic[2 * blocks[s] + part] = v.astype(BF16)

    far = {X: 1 - h}

    def x_copies(n, send, got):
        ends = [(near, 1 - h), (far, 1 - h), (pair, h)]
        return [
            remote(send.at[part], got.at[k], s_x.at[n, k], r_x.at[n, k], who)
            for k, (who, part) in enumerate(ends)
        ]

    x_i, x_o = x_copies(0, xi, xir), x_copies(1, xo, xor)

    def x_sum(copies, send, got):
        for copy in copies:
            copy.wait_recv()
        own, beside, across, mate = [v.astype(F32) for v in (send[h], got[0], got[1], got[2])]
        return (own + beside) + (mate + across)

    loss_copy(0).start()
    i_block(0)
    o_block(0)
    i_add(0)
    i1[0].begin()
    i_block(1)
    o_add(0)
    o1.start(0, 1)
    loss_next(0)
    o_block(1)
    i_add(1)
    i1[1].begin()
    i_block(2)
    o_add(1)
    o1.start(2)
    i1[0].middle()
    loss_next(1)
    i_block(3)
    i_add(2)
    i1[2].begin()
    o_block(2)
    i_add(3)
    i1[3].begin()
    i1[1].middle()
    o1.relay(0)
    loss_next(2)
    o_block(3)
    o_add(2)
    o1.start(3)
    o1.relay(1)
    i1[2].middle()
    i_end(0)
    o_add(3)
    i1[3].middle()
    i_end(1)
    loss_next(3)
    i_end(2)
    i_end(3)
    i2.begin()
    for part, v in enumerate(o1.end()):
        oc[:, 32 * part : 32 * part + 32] = v.astype(BF16)
    o2.begin()
    loss_next(4)
    i2.middle()
    o2.middle()
    loss_next(5)
    sums = i2.end()
    for half in range(2):
        for part in range(2):
            xi[half, 4 * part : 4 * part + 4] = sums[part][:, 8 * half : 8 * half + 8].astype(BF16)
    for copy in x_i:
        copy.start()
    for part, v in enumerate(o2.end()):
        xo[part] = v.astype(BF16)
    for copy in x_o:
        copy.start()
    loss_next(6)
    loss[0, 0] = jnp.sum(cr[7]) * (0.5 / float(2 * NODES * D))
    total = x_sum(x_i, xi, xir)
    for k in range(8):
        g_in[:, 256 * k : 256 * k + 256] = total[k]
    g_out[...] = x_sum(x_o, xo, xor)

    for copy in first_sends + x_i + x_o:
        copy.wait_send()
    for s in range(4):
        share(s, c).wait_send()
        for n in range(2):
            for half in range(2):
                core_copy(n, s, half).wait_send()
    for ring in i1 + [i2, o1, o2]:
        ring.drain()
    for t in range(TILES):
        store_own(t).wait()
        send_latents(t).wait_send()
        send_prediction(t).wait_send()
        remote(
            pbuf.at[1, pl.ds(t * TILE, TILE)],
            out.at[0, pl.ds(theirs + t * TILE, TILE)],
            s_prd.at[t],
            r_prd.at[t],
            pair,
        ).wait_recv()


def finish(p_in, gi_in, go_in, p_out, gi_out, go_out, held, s_in, s_out):
    def step(n, k):
        part = pl.ds(256 * k, 256)
        if n == 0:
            return pltpu.make_async_copy(p_in.at[0, part], held.at[part], s_in.at[k])
        return pltpu.make_async_copy(held.at[part], p_out.at[0, part], s_out.at[k])

    for k in range(8):
        step(0, k).start()
    gi_out[...] = gi_in[...]
    go_out[...] = go_in[...]
    for k in range(8):
        step(0, k).wait()
        step(1, k).start()
    for k in range(8):
        step(1, k).wait()


def vm(*shape, dtype=BF16):
    return pltpu.VMEM(shape, dtype)


def dma(*shape):
    return pltpu.SemaphoreType.DMA(shape)


SCRATCH = [
    vm(4, 4, 4, 32, 512), vm(4, 4, 4, 128, 128), vm(2, HALF, D), vm(HALF, D), vm(2, HALF, D),
    vm(2, HALF, D), vm(D, ROWS), vm(2, TILE, D), vm(D, ROWS), vm(4, ROWS, 512), vm(4, ROWS, 512), vm(1, 32, dtype=F32),
    vm(2, 8, 4, 4, 16, 256), vm(2, 4, 4, 64, 512), vm(8, 4, 4, 16, 256), vm(4, 4, 64, 512),
    vm(4, 4, 16, 256), vm(4, 4, 16, 256), vm(4, 2, 4, 16, 256), vm(4, 2, 4, 16, 256),
    vm(4, 32, 512), vm(4, 32, 512), vm(2, 4, 32, 512), vm(2, 4, 32, 512),
    vm(8, 4, 16, 256), vm(4, 64, 512),
    vm(4, 16, 256), vm(4, 16, 256), vm(2, 4, 16, 256), vm(2, 4, 16, 256),
    vm(32, 512), vm(32, 512), vm(2, 32, 512), vm(2, 32, 512),
    vm(2, 8, 8, 256), vm(3, 8, 8, 256), vm(2, 32, 512), vm(3, 32, 512),
    vm(8, 8, 128, dtype=F32), vm(7, 8, 128, dtype=F32),
    dma(TILES + 1), dma(TILES), dma(TILES), dma(TILES), dma(TILES), dma(TILES),
    pltpu.SemaphoreType.DMA, pltpu.SemaphoreType.DMA,
    dma(3, 4), dma(3, 4), dma(4), dma(4, 2, 4), dma(4, 2, 4), dma(4), dma(4), dma(2, 8), dma(2, 8),
    dma(7, 6), dma(7, 6), dma(2, 3), dma(2, 3), dma(7), dma(7),
]


def on_device(latents, noise, cond_gain, cond_shift, w_in, b_in, w_out, target):
    inside = pl.BlockSpec(memory_space=pltpu.VMEM)
    anywhere = pl.BlockSpec(memory_space=pl.ANY)
    prediction, grad_in, grad_out, loss = pl.pallas_call(
        kernel,
        out_shape=(
            jax.ShapeDtypeStruct((1, ROWS, D), BF16),
            jax.ShapeDtypeStruct((8, H), F32),
            jax.ShapeDtypeStruct((32, D), F32),
            jax.ShapeDtypeStruct((1, 1), F32),
        ),
        in_specs=[anywhere] + [inside] * 6 + [anywhere],
        out_specs=(anywhere, inside, inside, pl.BlockSpec(memory_space=pltpu.SMEM)),
        scratch_shapes=SCRATCH,
        compiler_params=pltpu.CompilerParams(
            collective_id=0, has_side_effects=True, vmem_limit_bytes=63 * 1024 * 1024
        ),
    )(latents, noise, cond_gain, cond_shift, w_in, b_in.reshape(1, H), w_out, target)
    prediction, grad_in, grad_out = pl.pallas_call(
        finish,
        out_shape=(
            jax.ShapeDtypeStruct((1, ROWS, D), BF16),
            jax.ShapeDtypeStruct((8, H), F32),
            jax.ShapeDtypeStruct((32, D), F32),
        ),
        in_specs=[anywhere, inside, inside],
        out_specs=(anywhere, inside, inside),
        scratch_shapes=[vm(ROWS, D), dma(8), dma(8)],
    )(prediction, grad_in, grad_out)
    return prediction, grad_in, grad_out, loss.reshape(())


def solution(mesh):
    torus = Mesh(mesh.devices.reshape(2, 4, 4, 2, 2), AXES)
    in_specs = (
        P(M, FSDP, None),
        P(M, None),
        P(),
        P(),
        P(FSDP, None),
        P(),
        P(FSDP, None),
        P(FSDP, None),
    )
    out_specs = (P(M, FSDP, None), P(FSDP, None), P(FSDP, None), P())
    return jax.shard_map(on_device, mesh=torus, in_specs=in_specs, out_specs=out_specs, check_vma=False)
```

time: 116 us -> 95.4 us (0.82)
  Pallas kernels: 108 us -> 92.4 us
  local copies, waits for them, and re-layouts: 5.65 us -> 0 us
    pallas_call x1, Pallas kernels: 108 us -> 88.4 us  [on_device(): pl.pallas_call(kernel, out_shape=(jax.ShapeDtypeStruct((1, ROWS, D), BF16...]
    unnamed x7 -> x0, local copies, waits for them, and re-layouts: 4.35 us -> none
    pallas_call x0 -> x1, Pallas kernels: none -> 3.92 us  [on_device(): pl.pallas_call(finish, out_shape=(jax.ShapeDtypeStruct((1, ROWS, D), BF16...]
    reshape x1 -> x0, local copies, waits for them, and re-layouts: 1.3 us -> none  [on_device(): b_in.reshape(4, 512)]
where the time goes in v2:
time: 95.4 us; the launch traced here: 94.8 us
  Pallas kernels  92.4 us (97%)
  between operations  2.39 us (3%)
    pallas_call x1, Pallas kernels, on_device(): pl.pallas_call(kernel, out_shape=(jax.ShapeDtypeStruct((1, ROWS, D), BF16...  88.4 us
    pallas_call x1, Pallas kernels, on_device(): pl.pallas_call(finish, out_shape=(jax.ShapeDtypeStruct((1, ROWS, D), BF16...  3.92 us

profile of v2, /device:TPU:0, one launch (start us, length us, event | category | flops | bytes accessed | tf_op | source)
XLA Modules:
  0.0 94.8 jit_solution(8873503102037340563)
XLA Ops:
  0.6 88.4 %shard_map.111 = (bf16[1,2048,512]{2,1,0:T(8,128)(2,1)}, f32[8,2048]{1,0:T(8,128)}, f32[32,512]{1,0:T(8,128)}, f32[1,1]{1,0:T(1,128)}) custom-call(bf16[1,2048,512]{2,1,0:T(8,128)(2,1)} %latents.1, f32[1,32]{1,0:T(1,128)} %noise.1, f32[32,512]{1,0:T(8,128)} %cond_gain.1, f32[32,512]{1,0:T(8,128)} %cond_shift.1, bf16[8,2048]{1,0:T(8,128)(2,1)} %w_in.1, ...), custom_call_target="tpu_custom_call" | custom-call | tf_op jit(solution)/shard_map/pallas_call | solution.py:594
  89.1 3.9 %shard_map.112 = (bf16[1,2048,512]{2,1,0:T(8,128)(2,1)}, f32[8,2048]{1,0:T(8,128)}, f32[32,512]{1,0:T(8,128)}) custom-call(bf16[1,2048,512]{2,1,0:T(8,128)(2,1)} %get-tuple-element.11.p_in, f32[8,2048]{1,0:T(8,128)} %get-tuple-element.12.gi_in, f32[32,512]{1,0:T(8,128)} %get-tuple-element.13.go_in), custom_call_target="tpu_custom_call" | custom-call | tf_op jit(solution)/shard_map/pallas_call | solution.py:609

commit v3 on v2

--- a/solution.py
+++ b/solution.py
@@ -1,5 +1,3 @@
-import functools
-
 import jax
 import jax.numpy as jnp
 from jax import lax
@@ -51,7 +49,7 @@
 def kernel(
     latents, noise, cond_gain, cond_shift, w_in, b_in, w_out, target,
     out, g_in, g_out, loss,
-    wi, wo, lat, tgt, pbuf, nrm, nt, dp, dt, act, slp, nz,
+    wi, wo, lat, tgt, pbuf, nrm, nt, dp0, dp1, dt, act, slp, nz,
     si, so, ri, ro, ihr, ihq, ifr, ifq, ohr, ohq, ofr, ofq,
     ic, oc, jhr, jhq, jfr, jfq, phr, phq, pfr, pfq,
     xi, xir, xo, xor, cr, crr,
@@ -61,6 +59,7 @@
     m, z, y, h, c = [lax.axis_index(a) for a in AXES]
     up = {Y: {Y: lax.rem(y + 1, 4)}, Z: {Z: lax.rem(z + 1, 4)}}
     down = {Y: {Y: lax.rem(y + 3, 4)}, Z: {Z: lax.rem(z + 3, 4)}}
+    away = {Y: {Y: lax.rem(y + 2, 4)}, Z: {Z: lax.rem(z + 2, 4)}}
     place = {Y: y, Z: z}
     sib = {C: 1 - c}
     pair = {M: 1 - m}
@@ -80,7 +79,7 @@
     load_target.start()
 
     barrier = pltpu.get_barrier_semaphore()
-    greeted = [sib, pair, near, cross, {X: 1 - h}, up[Y], down[Y], up[Z], down[Z]]
+    greeted = [sib, pair, near, cross, {X: 1 - h}, away[Y], away[Z], up[Y], down[Y], up[Z], down[Z]]
     for other in greeted:
         pl.semaphore_signal(barrier, inc=1, device_id=other, device_id_type=MESH)
     pl.semaphore_wait(barrier, len(greeted))
@@ -157,32 +156,39 @@
     def gather_copy(s, phase, n):
         axis = streams[s][2] if phase == 0 else other_axis(streams[s][2])
         p = place[axis]
-        i = [p, p, lax.rem(p + 3, 4), lax.rem(p + 1, 4)][n]
-        view = gather_view(s, phase, i, [None, None, 0, 1][n])
-        who = [up, down, up, down][n][axis]
+        if phase == 0:
+            i, part, who = p, None, [up, down, away][n][axis]
+        else:
+            i = [p, p, lax.rem(p + 3, 4), lax.rem(p + 1, 4)][n]
+            part, who = [None, None, 0, 1][n], [up, down, up, down][n][axis]
+        view = gather_view(s, phase, i, part)
         return remote(view, view, s_ag.at[s, phase, n], r_ag.at[s, phase, n], who)
 
     def gather_landed(s, phase, n):
         axis = streams[s][2] if phase == 0 else other_axis(streams[s][2])
         p = place[axis]
         i = lax.rem(p + [3, 1, 2, 2][n], 4)
-        view = gather_view(s, phase, i, [None, None, 0, 1][n])
+        view = gather_view(s, phase, i, None if phase == 0 else [None, None, 0, 1][n])
         remote(view, view, s_ag.at[s, phase, n], r_ag.at[s, phase, n], up[axis]).wait_recv()
 
     def gather_start(s, phase):
-        gather_copy(s, phase, 0).start()
-        gather_copy(s, phase, 1).start()
+        for n in range(3 if phase == 0 else 2):
+            gather_copy(s, phase, n).start()
 
     def gather_forward(s, phase):
+        if phase == 0:
+            return
         gather_landed(s, phase, 0)
         gather_copy(s, phase, 2).start()
         gather_landed(s, phase, 1)
         gather_copy(s, phase, 3).start()
 
     def gather_end(s, phase):
-        gather_landed(s, phase, 2)
-        gather_landed(s, phase, 3)
-        for n in range(4):
+        for n in range(3) if phase == 0 else (2, 3):
+            gather_landed(s, phase, n)
+
+    def gather_drain(s, phase):
+        for n in range(3 if phase == 0 else 4):
             gather_copy(s, phase, n).wait_send()
 
     def share(s, block_of):
@@ -273,10 +279,11 @@
     normalise(1, 2, other_gain, other_shift)
     lax.fori_loop(2, TILES, own_hidden, 0)
     normalise(1, 3, other_gain, other_shift)
-    lax.fori_loop(0, 2, partner_hidden, 0)
+    lax.fori_loop(0, 1, partner_hidden, 0)
     for s in range(2, 4):
         gather_end(s, 1)
         share(s, c).start()
+    lax.fori_loop(1, TILES, partner_hidden, 0)
     for s in range(2, 4):
         share(s, 1 - c).wait_recv()
     lax.fori_loop(0, TILES, own_out, 0)
@@ -285,37 +292,46 @@
     cr[0] = jnp.zeros((8, 128), F32)
     scale = float((2 * NODES) ** -0.5)
 
-    def both_tile(ready, t, carry):
+    def out_tile(t):
         x = lat[1, tile_of(0, t), :].astype(F32)
         for j in range(4):
-            a = act[j, tile_of(1, t), :] if ready else hidden(j, 1, t)
-            x = x + dot(a, w_out_rows(j))
+            x = x + dot(act[j, tile_of(1, t), :], w_out_rows(j))
         pbuf[1, tile_of(0, t), :] = x.astype(BF16)
         send_prediction(t).start()
-        rows = tile_of(0, t)
+
+    def loss_part(t, k):
+        rows = pl.ds(t * TILE + 128 * k, 128)
         p0 = pbuf[0, rows, :].astype(F32)
-        p1 = x.astype(BF16).astype(F32)
+        p1 = pbuf[1, rows, :].astype(F32)
         goal = tgt[rows, :].astype(F32)
         near0, near1, apart = p0 - goal, p1 - goal, p0 - p1
         q0, q1, qa = near0 * near0 + 0.0625, near1 * near1 + 0.0625, apart * apart + 0.0625
         i0, i1, ia = lax.rsqrt(q0), lax.rsqrt(q1), lax.rsqrt(qa)
         crps = q0 * i0 + q1 * i1 - qa * ia
-        summed = jnp.sum(crps.reshape(TILE // 8, 8, D), axis=0)
-        cr[0] += sum(summed[:, k * 128 : (k + 1) * 128] for k in range(4))
+        summed = jnp.sum(crps.reshape(16, 8, D), axis=0)
+        cr[0] += sum(summed[:, n * 128 : (n + 1) * 128] for n in range(4))
         pull = (0.5 * scale) * (apart * ia)
         grads = ((0.5 * scale) * (near0 * i0) - pull, (0.5 * scale) * (near1 * i1) + pull)
         for slot in range(2):
-            dp[slot] = grads[slot].astype(BF16)
-            dt[:, tile_of(slot, t)] = grads[slot].T.astype(BF16)
+            at = slot * TILE + 128 * k
+            (dp0, dp1)[t % 2][at : at + 128, :] = grads[slot].astype(BF16)
+            dt[:, pl.ds(slot * HALF + t * TILE + 128 * k, 128)] = grads[slot].T.astype(BF16)
+
+    def back(t, j):
+        dact = dot_t((dp0, dp1)[t % 2][...], w_out_rows(j))
+        for slot in range(2):
+            at = tile_of(slot, t)
+            part = dact[slot * TILE : slot * TILE + TILE]
+            slp[j, at, :] = (part * slp[j, at, :].astype(F32)).astype(BF16)
+
+    for t in range(TILES + 1):
+        if t < TILES:
+            out_tile(t)
         for j in range(4):
-            w = w_out_rows(j)
-            for slot in range(2):
-                at = tile_of(slot, t)
-                slp[j, at, :] = (dot_t(dp[slot], w) * slp[j, at, :].astype(F32)).astype(BF16)
-        return carry
-
-    lax.fori_loop(0, 2, functools.partial(both_tile, True), 0)
-    lax.fori_loop(2, TILES, functools.partial(both_tile, False), 0)
+            if t > 0:
+                back(t - 1, j)
+            if t < TILES and j < 2:
+                loss_part(t, j)
 
     mates = [
         sib,
@@ -460,38 +476,38 @@
         return (own + beside) + (mate + across)
 
     loss_copy(0).start()
+    o_block(0)
     i_block(0)
-    o_block(0)
+    o_add(0)
+    o1.start(0, 1)
+    i_block(1)
     i_add(0)
     i1[0].begin()
-    i_block(1)
-    o_add(0)
-    o1.start(0, 1)
-    loss_next(0)
-    o_block(1)
+    i_block(2)
     i_add(1)
     i1[1].begin()
-    i_block(2)
-    o_add(1)
-    o1.start(2)
-    i1[0].middle()
-    loss_next(1)
+    loss_next(0)
     i_block(3)
     i_add(2)
     i1[2].begin()
-    o_block(2)
+    o_block(1)
     i_add(3)
     i1[3].begin()
+    loss_next(1)
+    o_block(2)
+    i1[0].middle()
+    o_add(1)
+    o1.start(2)
+    o1.relay(0)
+    o_block(3)
     i1[1].middle()
-    o1.relay(0)
-    loss_next(2)
-    o_block(3)
     o_add(2)
     o1.start(3)
     o1.relay(1)
+    loss_next(2)
     i1[2].middle()
+    o_add(3)
     i_end(0)
-    o_add(3)
     i1[3].middle()
     i_end(1)
     loss_next(3)
@@ -525,6 +541,8 @@
     for copy in first_sends + x_i + x_o:
         copy.wait_send()
     for s in range(4):
+        gather_drain(s, 0)
+        gather_drain(s, 1)
         share(s, c).wait_send()
         for n in range(2):
             for half in range(2):
@@ -544,22 +562,20 @@
         ).wait_recv()
 
 
-def finish(p_in, gi_in, go_in, p_out, gi_out, go_out, held, s_in, s_out):
-    def step(n, k):
+def finish(p_in, gi_in, go_in, p_out, gi_out, go_out, held, gi, go, s_in, s_out):
+    routes = [(gi_in, gi, gi_out), (go_in, go, go_out)]
+    for k in range(8):
         part = pl.ds(256 * k, 256)
-        if n == 0:
-            return pltpu.make_async_copy(p_in.at[0, part], held.at[part], s_in.at[k])
-        return pltpu.make_async_copy(held.at[part], p_out.at[0, part], s_out.at[k])
-
-    for k in range(8):
-        step(0, k).start()
-    gi_out[...] = gi_in[...]
-    go_out[...] = go_in[...]
-    for k in range(8):
-        step(0, k).wait()
-        step(1, k).start()
-    for k in range(8):
-        step(1, k).wait()
+        routes.append((p_in.at[0, part], held.at[part], p_out.at[0, part]))
+    loads = [pltpu.make_async_copy(a, b, s_in.at[k]) for k, (a, b, _) in enumerate(routes)]
+    stores = [pltpu.make_async_copy(b, d, s_out.at[k]) for k, (_, b, d) in enumerate(routes)]
+    for load in loads:
+        load.start()
+    for load, store in zip(loads, stores):
+        load.wait()
+        store.start()
+    for store in stores:
+        store.wait()
 
 
 def vm(*shape, dtype=BF16):
@@ -572,7 +588,7 @@
 
 SCRATCH = [
     vm(4, 4, 4, 32, 512), vm(4, 4, 4, 128, 128), vm(2, HALF, D), vm(HALF, D), vm(2, HALF, D),
-    vm(2, HALF, D), vm(D, ROWS), vm(2, TILE, D), vm(D, ROWS), vm(4, ROWS, 512), vm(4, ROWS, 512), vm(1, 32, dtype=F32),
+    vm(2, HALF, D), vm(D, ROWS), vm(2 * TILE, D), vm(2 * TILE, D), vm(D, ROWS), vm(4, ROWS, 512), vm(4, ROWS, 512), vm(1, 32, dtype=F32),
     vm(2, 8, 4, 4, 16, 256), vm(2, 4, 4, 64, 512), vm(8, 4, 4, 16, 256), vm(4, 4, 64, 512),
     vm(4, 4, 16, 256), vm(4, 4, 16, 256), vm(4, 2, 4, 16, 256), vm(4, 2, 4, 16, 256),
     vm(4, 32, 512), vm(4, 32, 512), vm(2, 4, 32, 512), vm(2, 4, 32, 512),
@@ -613,9 +629,9 @@
             jax.ShapeDtypeStruct((8, H), F32),
             jax.ShapeDtypeStruct((32, D), F32),
         ),
-        in_specs=[anywhere, inside, inside],
-        out_specs=(anywhere, inside, inside),
-        scratch_shapes=[vm(ROWS, D), dma(8), dma(8)],
+        in_specs=[anywhere] * 3,
+        out_specs=(anywhere,) * 3,
+        scratch_shapes=[vm(ROWS, D), vm(8, H, dtype=F32), vm(32, D, dtype=F32), dma(10), dma(10)],
     )(prediction, grad_in, grad_out)
     return prediction, grad_in, grad_out, loss.reshape(())
 

time: 95.4 us -> 89.9 us (0.942)
  Pallas kernels: 92.4 us -> 87.3 us
    pallas_call x1, Pallas kernels: 88.4 us -> 84.8 us  [on_device(): pl.pallas_call(kernel, out_shape=(jax.ShapeDtypeStruct((1, ROWS, D), BF16...]
    pallas_call x1, Pallas kernels: 3.92 us -> 2.51 us  [on_device(): pl.pallas_call(finish, out_shape=(jax.ShapeDtypeStruct((1, ROWS, D), BF16...]
where the time goes in v3:
time: 89.9 us; the launch traced here: 89.7 us
  Pallas kernels  87.3 us (97%)
  between operations  2.39 us (3%)
    pallas_call x1, Pallas kernels, on_device(): pl.pallas_call(kernel, out_shape=(jax.ShapeDtypeStruct((1, ROWS, D), BF16...  84.8 us
    pallas_call x1, Pallas kernels, on_device(): pl.pallas_call(finish, out_shape=(jax.ShapeDtypeStruct((1, ROWS, D), BF16...  2.51 us

profile of v3, /device:TPU:0, one launch (start us, length us, event | category | flops | bytes accessed | tf_op | source)
XLA Modules:
  0.0 89.7 jit_solution(8548568794834935834)
XLA Ops:
  0.6 84.8 %shard_map.111 = (bf16[1,2048,512]{2,1,0:T(8,128)(2,1)}, f32[8,2048]{1,0:T(8,128)}, f32[32,512]{1,0:T(8,128)}, f32[1,1]{1,0:T(1,128)}) custom-call(bf16[1,2048,512]{2,1,0:T(8,128)(2,1)} %latents.1, f32[1,32]{1,0:T(1,128)} %noise.1, f32[32,512]{1,0:T(8,128)} %cond_gain.1, f32[32,512]{1,0:T(8,128)} %cond_shift.1, bf16[8,2048]{1,0:T(8,128)(2,1)} %w_in.1, ...), custom_call_target="tpu_custom_call" | custom-call | tf_op jit(solution)/shard_map/pallas_call | solution.py:610
  85.4 2.5 %shard_map.112 = (bf16[1,2048,512]{2,1,0:T(8,128)(2,1)}, f32[8,2048]{1,0:T(8,128)}, f32[32,512]{1,0:T(8,128)}) custom-call(bf16[1,2048,512]{2,1,0:T(8,128)(2,1)} %get-tuple-element.11.p_in, f32[8,2048]{1,0:T(8,128)} %get-tuple-element.12.gi_in, f32[32,512]{1,0:T(8,128)} %get-tuple-element.13.go_in), custom_call_target="tpu_custom_call" | custom-call | tf_op jit(solution)/shard_map/pallas_call | solution.py:625

commit v4 on v3

--- a/solution.py
+++ b/solution.py
@@ -265,28 +265,29 @@
             hidden(j, 1, t)
         return carry
 
-    def own_out(t, carry):
+    def own_out(t, beside):
         x = lat[0, tile_of(0, t), :].astype(F32)
         for j in range(4):
             x = x + dot(act[j, tile_of(0, t), :], w_out_rows(j))
+            if beside is not None:
+                hidden(j, 1, beside)
         pbuf[0, tile_of(0, t), :] = x.astype(BF16)
         store_own(t).start()
-        return carry
-
-    lax.fori_loop(0, 2, own_hidden, 0)
+
+    lax.fori_loop(0, 1, own_hidden, 0)
     for s in range(2, 4):
         gather_forward(s, 1)
-    normalise(1, 2, other_gain, other_shift)
-    lax.fori_loop(2, TILES, own_hidden, 0)
-    normalise(1, 3, other_gain, other_shift)
-    lax.fori_loop(0, 1, partner_hidden, 0)
+    lax.fori_loop(1, TILES, own_hidden, 0)
+    for t in range(2, TILES):
+        normalise(1, t, other_gain, other_shift)
     for s in range(2, 4):
         gather_end(s, 1)
         share(s, c).start()
-    lax.fori_loop(1, TILES, partner_hidden, 0)
+    lax.fori_loop(0, 2, partner_hidden, 0)
     for s in range(2, 4):
         share(s, 1 - c).wait_recv()
-    lax.fori_loop(0, TILES, own_out, 0)
+    for t in range(TILES):
+        own_out(t, t + 2 if t + 2 < TILES else None)
 
     load_target.wait()
     cr[0] = jnp.zeros((8, 128), F32)
@@ -486,32 +487,32 @@
     i_block(2)
     i_add(1)
     i1[1].begin()
-    loss_next(0)
     i_block(3)
     i_add(2)
     i1[2].begin()
+    loss_next(0)
     o_block(1)
     i_add(3)
     i1[3].begin()
-    loss_next(1)
     o_block(2)
-    i1[0].middle()
     o_add(1)
     o1.start(2)
+    i1[0].middle()
     o1.relay(0)
+    loss_next(1)
     o_block(3)
-    i1[1].middle()
     o_add(2)
     o1.start(3)
     o1.relay(1)
-    loss_next(2)
+    i1[1].middle()
     i1[2].middle()
     o_add(3)
+    i1[3].middle()
+    loss_next(2)
     i_end(0)
-    i1[3].middle()
     i_end(1)
+    i_end(2)
     loss_next(3)
-    i_end(2)
     i_end(3)
     i2.begin()
     for part, v in enumerate(o1.end()):

time: 89.9 us -> 88.3 us (0.982)
  Pallas kernels: 87.3 us -> 85.8 us
    pallas_call x1, Pallas kernels: 84.8 us -> 83.2 us  [on_device(): pl.pallas_call(kernel, out_shape=(jax.ShapeDtypeStruct((1, ROWS, D), BF16...]
where the time goes in v4:
time: 88.3 us; the launch traced here: 88.1 us
  Pallas kernels  85.8 us (97%)
  between operations  2.39 us (3%)
    pallas_call x1, Pallas kernels, on_device(): pl.pallas_call(kernel, out_shape=(jax.ShapeDtypeStruct((1, ROWS, D), BF16...  83.2 us
    pallas_call x1, Pallas kernels, on_device(): pl.pallas_call(finish, out_shape=(jax.ShapeDtypeStruct((1, ROWS, D), BF16...  2.51 us

profile of v4, /device:TPU:0, one launch (start us, length us, event | category | flops | bytes accessed | tf_op | source)
XLA Modules:
  0.0 88.1 jit_solution(509465488581865322)
XLA Ops:
  0.6 83.2 %shard_map.111 = (bf16[1,2048,512]{2,1,0:T(8,128)(2,1)}, f32[8,2048]{1,0:T(8,128)}, f32[32,512]{1,0:T(8,128)}, f32[1,1]{1,0:T(1,128)}) custom-call(bf16[1,2048,512]{2,1,0:T(8,128)(2,1)} %latents.1, f32[1,32]{1,0:T(1,128)} %noise.1, f32[32,512]{1,0:T(8,128)} %cond_gain.1, f32[32,512]{1,0:T(8,128)} %cond_shift.1, bf16[8,2048]{1,0:T(8,128)(2,1)} %w_in.1, ...), custom_call_target="tpu_custom_call" | custom-call | tf_op jit(solution)/shard_map/pallas_call | solution.py:611
  83.9 2.5 %shard_map.112 = (bf16[1,2048,512]{2,1,0:T(8,128)(2,1)}, f32[8,2048]{1,0:T(8,128)}, f32[32,512]{1,0:T(8,128)}) custom-call(bf16[1,2048,512]{2,1,0:T(8,128)(2,1)} %get-tuple-element.11.p_in, f32[8,2048]{1,0:T(8,128)} %get-tuple-element.12.gi_in, f32[32,512]{1,0:T(8,128)} %get-tuple-element.13.go_in), custom_call_target="tpu_custom_call" | custom-call | tf_op jit(solution)/shard_map/pallas_call | solution.py:626

commit v5 on v4

--- a/solution.py
+++ b/solution.py
@@ -51,7 +51,7 @@
     out, g_in, g_out, loss,
     wi, wo, lat, tgt, pbuf, nrm, nt, dp0, dp1, dt, act, slp, nz,
     si, so, ri, ro, ihr, ihq, ifr, ifq, ohr, ohq, ofr, ofq,
-    ic, oc, jhr, jhq, jfr, jfq, phr, phq, pfr, pfq,
+    ic, oc, jgot, pgot,
     xi, xir, xo, xor, cr, crr,
     s_ld, s_out, s_lat, r_lat, s_prd, r_prd, s_nz, r_nz,
     s_w0, r_w0, l_w0, s_ag, r_ag, s_sib, r_sib, s_core, r_core, s_rs, r_rs, s_x, r_x, s_cr, r_cr,
@@ -444,6 +444,30 @@
             for k in range(6):
                 self.move(k).wait_send()
 
+    class Direct:
+        def __init__(self, n, axis, view, got):
+            p = place[axis]
+            self.view, self.p, self.got = view, p, got
+            ends = [(2, away), (1, up), (3, down)]
+            self.copies = [
+                remote(view(lax.rem(p + d, 4)), got.at[k], s_rs.at[n, k], r_rs.at[n, k], who[axis])
+                for k, (d, who) in enumerate(ends)
+            ]
+
+        def begin(self):
+            for copy in self.copies:
+                copy.start()
+
+        def end(self):
+            for copy in self.copies:
+                copy.wait_recv()
+            own, *others = [v.astype(F32) for v in (self.view(self.p)[...], *[self.got[k] for k in range(3)])]
+            return (own + others[0]) + (others[1] + others[2])
+
+        def drain(self):
+            for copy in self.copies:
+                copy.wait_send()
+
     def i_ring(s):
         return Ring(
             s, Y, lambda i, part: si.at[c, 2 * blocks[s] + part, :, i],
@@ -451,9 +475,9 @@
         )
 
     i1 = [i_ring(s) for s in range(4)]
-    i2 = Ring(4, Z, lambda i, part: ic.at[pl.ds(4 * part, 4), i], jhr, jhq, jfr, jfq)
+    i2 = Direct(4, Z, lambda i: ic.at[:, i], jgot)
     o1 = Ring(5, Z, lambda i, part: so.at[c, i, :, pl.ds(32 * part, 32)], ohr, ohq, ofr, ofq)
-    o2 = Ring(6, Y, lambda i, part: oc.at[i, pl.ds(32 * part, 32)], phr, phq, pfr, pfq)
+    o2 = Direct(6, Y, lambda i: oc.at[i], pgot)
 
     def i_end(s):
         for part, v in enumerate(i1[s].end()):
@@ -519,17 +543,15 @@
         oc[:, 32 * part : 32 * part + 32] = v.astype(BF16)
     o2.begin()
     loss_next(4)
-    i2.middle()
-    o2.middle()
     loss_next(5)
     sums = i2.end()
     for half in range(2):
-        for part in range(2):
-            xi[half, 4 * part : 4 * part + 4] = sums[part][:, 8 * half : 8 * half + 8].astype(BF16)
+        xi[half] = sums[:, 8 * half : 8 * half + 8].astype(BF16)
     for copy in x_i:
         copy.start()
-    for part, v in enumerate(o2.end()):
-        xo[part] = v.astype(BF16)
+    sums = o2.end()
+    for half in range(2):
+        xo[half] = sums[32 * half : 32 * half + 32].astype(BF16)
     for copy in x_o:
         copy.start()
     loss_next(6)
@@ -594,8 +616,7 @@
     vm(4, 4, 16, 256), vm(4, 4, 16, 256), vm(4, 2, 4, 16, 256), vm(4, 2, 4, 16, 256),
     vm(4, 32, 512), vm(4, 32, 512), vm(2, 4, 32, 512), vm(2, 4, 32, 512),
     vm(8, 4, 16, 256), vm(4, 64, 512),
-    vm(4, 16, 256), vm(4, 16, 256), vm(2, 4, 16, 256), vm(2, 4, 16, 256),
-    vm(32, 512), vm(32, 512), vm(2, 32, 512), vm(2, 32, 512),
+    vm(3, 8, 16, 256), vm(3, 64, 512),
     vm(2, 8, 8, 256), vm(3, 8, 8, 256), vm(2, 32, 512), vm(3, 32, 512),
     vm(8, 8, 128, dtype=F32), vm(7, 8, 128, dtype=F32),
     dma(TILES + 1), dma(TILES), dma(TILES), dma(TILES), dma(TILES), dma(TILES),

time: 88.3 us -> 86.9 us (0.984)
  Pallas kernels: 85.8 us -> 84.3 us
    pallas_call x1, Pallas kernels: 83.2 us -> 81.8 us  [on_device(): pl.pallas_call(kernel, out_shape=(jax.ShapeDtypeStruct((1, ROWS, D), BF16...]
where the time goes in v5:
time: 86.9 us; the launch traced here: 86.7 us
  Pallas kernels  84.3 us (97%)
  between operations  2.39 us (3%)
    pallas_call x1, Pallas kernels, on_device(): pl.pallas_call(kernel, out_shape=(jax.ShapeDtypeStruct((1, ROWS, D), BF16...  81.8 us
    pallas_call x1, Pallas kernels, on_device(): pl.pallas_call(finish, out_shape=(jax.ShapeDtypeStruct((1, ROWS, D), BF16...  2.51 us

profile of v5, /device:TPU:0, one launch (start us, length us, event | category | flops | bytes accessed | tf_op | source)
XLA Modules:
  0.0 86.7 jit_solution(3783410925730908347)
XLA Ops:
  0.6 81.8 %shard_map.111 = (bf16[1,2048,512]{2,1,0:T(8,128)(2,1)}, f32[8,2048]{1,0:T(8,128)}, f32[32,512]{1,0:T(8,128)}, f32[1,1]{1,0:T(1,128)}) custom-call(bf16[1,2048,512]{2,1,0:T(8,128)(2,1)} %latents.1, f32[1,32]{1,0:T(1,128)} %noise.1, f32[32,512]{1,0:T(8,128)} %cond_gain.1, f32[32,512]{1,0:T(8,128)} %cond_shift.1, bf16[8,2048]{1,0:T(8,128)(2,1)} %w_in.1, ...), custom_call_target="tpu_custom_call" | custom-call | tf_op jit(solution)/shard_map/pallas_call | solution.py:632
  82.4 2.5 %shard_map.112 = (bf16[1,2048,512]{2,1,0:T(8,128)(2,1)}, f32[8,2048]{1,0:T(8,128)}, f32[32,512]{1,0:T(8,128)}) custom-call(bf16[1,2048,512]{2,1,0:T(8,128)(2,1)} %get-tuple-element.11.p_in, f32[8,2048]{1,0:T(8,128)} %get-tuple-element.12.gi_in, f32[32,512]{1,0:T(8,128)} %get-tuple-element.13.go_in), custom_call_target="tpu_custom_call" | custom-call | tf_op jit(solution)/shard_map/pallas_call | solution.py:647

commit v6 on v5

--- a/solution.py
+++ b/solution.py
@@ -51,7 +51,7 @@
     out, g_in, g_out, loss,
     wi, wo, lat, tgt, pbuf, nrm, nt, dp0, dp1, dt, act, slp, nz,
     si, so, ri, ro, ihr, ihq, ifr, ifq, ohr, ohq, ofr, ofq,
-    ic, oc, jgot, pgot,
+    ic, oc, jgot, pgot, lgot,
     xi, xir, xo, xor, cr, crr,
     s_ld, s_out, s_lat, r_lat, s_prd, r_prd, s_nz, r_nz,
     s_w0, r_w0, l_w0, s_ag, r_ag, s_sib, r_sib, s_core, r_core, s_rs, r_rs, s_x, r_x, s_cr, r_cr,
@@ -474,14 +474,16 @@
             ihr.at[s], ihq.at[s], ifr.at[s], ifq.at[s],
         )
 
-    i1 = [i_ring(s) for s in range(4)]
+    i1 = [i_ring(s) for s in range(3)]
+    i1.append(Direct(3, Y, lambda i: si.at[c, pl.ds(2 * blocks[3], 2), :, i], lgot))
     i2 = Direct(4, Z, lambda i: ic.at[:, i], jgot)
     o1 = Ring(5, Z, lambda i, part: so.at[c, i, :, pl.ds(32 * part, 32)], ohr, ohq, ofr, ofq)
     o2 = Direct(6, Y, lambda i: oc.at[i], pgot)
 
     def i_end(s):
-        for part, v in enumerate(i1[s].end()):
-            ic[2 * blocks[s] + part] = v.astype(BF16)
+        sums = i1[s].end()
+        for part in range(2):
+            ic[2 * blocks[s] + part] = sums[part].astype(BF16)
 
     far = {X: 1 - h}
 
@@ -511,27 +513,26 @@
     i_block(2)
     i_add(1)
     i1[1].begin()
-    i_block(3)
+    o_block(1)
     i_add(2)
     i1[2].begin()
     loss_next(0)
-    o_block(1)
-    i_add(3)
-    i1[3].begin()
     o_block(2)
     o_add(1)
     o1.start(2)
+    i_block(3)
+    o_add(2)
+    o1.start(3)
     i1[0].middle()
     o1.relay(0)
     loss_next(1)
     o_block(3)
-    o_add(2)
-    o1.start(3)
+    i_add(3)
+    i1[3].begin()
     o1.relay(1)
     i1[1].middle()
     i1[2].middle()
     o_add(3)
-    i1[3].middle()
     loss_next(2)
     i_end(0)
     i_end(1)
@@ -616,7 +617,7 @@
     vm(4, 4, 16, 256), vm(4, 4, 16, 256), vm(4, 2, 4, 16, 256), vm(4, 2, 4, 16, 256),
     vm(4, 32, 512), vm(4, 32, 512), vm(2, 4, 32, 512), vm(2, 4, 32, 512),
     vm(8, 4, 16, 256), vm(4, 64, 512),
-    vm(3, 8, 16, 256), vm(3, 64, 512),
+    vm(3, 8, 16, 256), vm(3, 64, 512), vm(3, 2, 4, 16, 256),
     vm(2, 8, 8, 256), vm(3, 8, 8, 256), vm(2, 32, 512), vm(3, 32, 512),
     vm(8, 8, 128, dtype=F32), vm(7, 8, 128, dtype=F32),
     dma(TILES + 1), dma(TILES), dma(TILES), dma(TILES), dma(TILES), dma(TILES),

time: 86.9 us -> 87.3 us (level)
  no operation moved by 1% of the time
where the time goes in v6:
time: 87.3 us; the launch traced here: 87 us
  Pallas kernels  84.7 us (97%)
  between operations  2.39 us (3%)
    pallas_call x1, Pallas kernels, on_device(): pl.pallas_call(kernel, out_shape=(jax.ShapeDtypeStruct((1, ROWS, D), BF16...  82.1 us
    pallas_call x1, Pallas kernels, on_device(): pl.pallas_call(finish, out_shape=(jax.ShapeDtypeStruct((1, ROWS, D), BF16...  2.51 us

profile of v6, /device:TPU:0, one launch (start us, length us, event | category | flops | bytes accessed | tf_op | source)
XLA Modules:
  0.0 87.0 jit_solution(9085703975182836036)
XLA Ops:
  0.6 82.1 %shard_map.111 = (bf16[1,2048,512]{2,1,0:T(8,128)(2,1)}, f32[8,2048]{1,0:T(8,128)}, f32[32,512]{1,0:T(8,128)}, f32[1,1]{1,0:T(1,128)}) custom-call(bf16[1,2048,512]{2,1,0:T(8,128)(2,1)} %latents.1, f32[1,32]{1,0:T(1,128)} %noise.1, f32[32,512]{1,0:T(8,128)} %cond_gain.1, f32[32,512]{1,0:T(8,128)} %cond_shift.1, bf16[8,2048]{1,0:T(8,128)(2,1)} %w_in.1, ...), custom_call_target="tpu_custom_call" | custom-call | tf_op jit(solution)/shard_map/pallas_call | solution.py:633
  82.8 2.5 %shard_map.112 = (bf16[1,2048,512]{2,1,0:T(8,128)(2,1)}, f32[8,2048]{1,0:T(8,128)}, f32[32,512]{1,0:T(8,128)}) custom-call(bf16[1,2048,512]{2,1,0:T(8,128)(2,1)} %get-tuple-element.11.p_in, f32[8,2048]{1,0:T(8,128)} %get-tuple-element.12.gi_in, f32[32,512]{1,0:T(8,128)} %get-tuple-element.13.go_in), custom_call_target="tpu_custom_call" | custom-call | tf_op jit(solution)/shard_map/pallas_call | solution.py:648
